TPU v7x, 32 devices: a whole 2x2x4 slice. The times are simulated.
32 devices in a mesh: leg: 2 (over y), ping: 8 (over z, core), rng: 2 (over x).
Axes of the slice: x: 2, y: 2, z: 4, core: 2. Of those that a mesh axis runs over, the one named last changes fastest.
Arguments:
- echo: bfloat16 [2, 16384, 256], P(None, ('leg', 'ping'), 'rng'), parts along dimension 1, may hold values from -6 to 6
- steer: bfloat16 [2, 16384, 8192], P(None, ('leg', 'rng'), 'ping'), parts along dimension 1, may hold values from -0.046875 to 0.046875
- offsets: int32 [256], P(('leg', 'ping')), parts along dimension 0, may hold values from 0 to 15
- taps: float32 [256, 4], P(('leg', 'ping')), parts along dimension 0, may hold values from 0.1 to 1
- centers: int32 [512], P(('leg', 'ping', 'rng')), parts along dimension 0, may hold values from 0 to 8191
- halves: int32 [512], P(('leg', 'ping', 'rng')), parts along dimension 0, may hold values from 128 to 1024
Outputs:
- focused: float32 [2, 512, 8192], P(None, ('leg', 'ping', 'rng')), parts along dimension 1
- phase_error: float32 [16384], P('leg'), parts along dimension 0
There are 2 independent parts, one for each index of `leg`. A program takes and returns all parts, laid end to end along the dimension named above; each array names one. Nothing has to cross between parts.
All inputs are finite; a program needn't handle non-finite values.
Results may differ from a plain program's by a relative error of at most 0.0049.
Values may be sent and summed in bfloat16 or wider, within the bound.
A program may use at most 64 MiB of HBM per device.

v0:
```python
import functools
import math

import jax
import jax.numpy as jnp
from jax import lax
from jax.experimental import pallas as pl
from jax.experimental.pallas import tpu as pltpu
from jax.sharding import PartitionSpec as P

PBLK = 64
NTAP = 4


epsilon = 1e-06


MESH = pl.DeviceIdType.MESH


def meet(peers):
    barrier = pltpu.get_barrier_semaphore()
    for peer in peers:
        pl.semaphore_signal(barrier, inc=1, device_id=peer, device_id_type=MESH)
    pl.semaphore_wait(barrier, len(peers))


def interp_kernel(tiles, offsets_ref, taps_ref, echo_ref, out_ref, held, send_sem, recv_sem, own_sem):
    me = lax.axis_index("rng")
    columns = echo_ref.shape[2]
    width = tiles * columns
    own = pltpu.make_async_copy(echo_ref, held.at[me], own_sem)
    own.start()
    peers = [{"rng": lax.rem(me + step, tiles)} for step in range(1, tiles)]
    meet(peers)
    copies = []
    for step, peer in enumerate(peers):
        copy = pltpu.make_async_remote_copy(
            src_ref=echo_ref,
            dst_ref=held.at[me],
            send_sem=send_sem.at[step],
            recv_sem=recv_sem.at[step],
            device_id=peer,
            device_id_type=MESH,
        )
        copy.start()
        copies.append(copy)
    own.wait()
    for copy in copies:
        copy.wait()

    def block(index, carry):
        rows = pl.ds(pl.multiple_of(index * PBLK, PBLK), PBLK)
        offset = offsets_ref[index]
        for part in range(2):
            value = jnp.concatenate([held[tile, part, rows, :] for tile in range(tiles)], axis=1)
            value = value.astype(jnp.float32)
            column = lax.broadcasted_iota(jnp.int32, (PBLK, width), 1)
            result = jnp.zeros((PBLK, width), jnp.float32)
            for tap in range(NTAP):
                shift = offset + tap
                moved = jnp.where(column >= shift, pltpu.roll(value, shift, axis=1), 0.0)
                result = result + taps_ref[index, tap] * moved
            out_ref[part, rows, :] = result.astype(jnp.bfloat16)
        return carry

    lax.fori_loop(0, out_ref.shape[1] // PBLK, block, 0)


def gather_interp(echo, offsets, taps):
    tiles = lax.axis_size("rng")
    rows, columns = echo.shape[1:]
    vmem = pl.BlockSpec(memory_space=pltpu.VMEM)
    smem = pl.BlockSpec(memory_space=pltpu.SMEM)
    return pl.pallas_call(
        functools.partial(interp_kernel, tiles),
        out_shape=jax.ShapeDtypeStruct((2, rows, tiles * columns), jnp.bfloat16),
        in_specs=[smem, smem, vmem],
        out_specs=vmem,
        scratch_shapes=[
            pltpu.VMEM((tiles, 2, rows, columns), jnp.bfloat16),
            pltpu.SemaphoreType.DMA((tiles - 1,)),
            pltpu.SemaphoreType.DMA((tiles - 1,)),
            pltpu.SemaphoreType.DMA,
        ],
        compiler_params=pltpu.CompilerParams(
            collective_id=0, has_side_effects=True, vmem_limit_bytes=48 * 2**20
        ),
    )(offsets, taps, echo)


def total_kernel(pings, tiles, value_ref, out_ref, held, full, send_sem, recv_sem, send_two, recv_two):
    count = pings * tiles
    me = lax.axis_index("ping") * tiles + lax.axis_index("rng")
    ids = [lax.rem(me + step, count) for step in range(1, count)]
    peers = [{"ping": lax.div(one, tiles), "rng": lax.rem(one, tiles)} for one in ids]
    meet(peers)
    copies = []
    for step, peer in enumerate(peers):
        copy = pltpu.make_async_remote_copy(
            src_ref=value_ref.at[ids[step]],
            dst_ref=held.at[step],
            send_sem=send_sem.at[step],
            recv_sem=recv_sem.at[step],
            device_id=peer,
            device_id_type=MESH,
        )
        copy.start()
        copies.append(copy)
    total = value_ref[me]
    for step, copy in enumerate(copies):
        copy.wait()
        total = total + held[step]
    full[me] = total
    copies = []
    for step, peer in enumerate(peers):
        copy = pltpu.make_async_remote_copy(
            src_ref=full.at[me],
            dst_ref=full.at[me],
            send_sem=send_two.at[step],
            recv_sem=recv_two.at[step],
            device_id=peer,
            device_id_type=MESH,
        )
        copy.start()
        copies.append(copy)
    for copy in copies:
        copy.wait()
    out_ref[...] = full[...]


def total_over(first, second):
    pings, tiles = lax.axis_size("ping"), lax.axis_size("rng")
    count = pings * tiles
    length = first.shape[0]
    value = jnp.concatenate([first, second]).reshape(count, -1, 128)
    vmem = pl.BlockSpec(memory_space=pltpu.VMEM)
    semaphores = pltpu.SemaphoreType.DMA((count - 1,))
    total = pl.pallas_call(
        functools.partial(total_kernel, pings, tiles),
        out_shape=jax.ShapeDtypeStruct(value.shape, jnp.float32),
        in_specs=[vmem],
        out_specs=vmem,
        scratch_shapes=[
            pltpu.VMEM((count - 1,) + value.shape[1:], jnp.float32),
            pltpu.VMEM(value.shape, jnp.float32),
            semaphores,
            semaphores,
            semaphores,
            semaphores,
        ],
        compiler_params=pltpu.CompilerParams(collective_id=1, has_side_effects=True),
    )(value).reshape(2, length)
    return total[0], total[1]


def split_length(length):
    factor_low = 1
    candidate = 1
    while candidate * candidate <= length:
        if length % candidate == 0:
            factor_low = candidate
        candidate = candidate + 1
    return factor_low


def table(rows_count, cols_count, modulus, direction):
    row_ids = jnp.arange(rows_count, dtype=jnp.int32)
    col_ids = jnp.arange(cols_count, dtype=jnp.int32)
    product = row_ids[:, None] * col_ids[None, :] % modulus
    angle = direction * 2.0 * math.pi / modulus * product.astype(jnp.float32)
    return (jnp.cos(angle), jnp.sin(angle))


def transform(real_part, imag_part, direction):
    length = real_part.shape[-1]
    size_low = split_length(length)
    size_high = length // size_low
    lead_shape = real_part.shape[:-1]
    highest = lax.Precision.HIGHEST
    real_grid = real_part.reshape(lead_shape + (size_low, size_high))
    imag_grid = imag_part.reshape(lead_shape + (size_low, size_high))
    first_cos, first_sin = table(size_low, size_low, size_low, direction)
    section_real = jnp.einsum(
        "kn,...nm->...km", first_cos, real_grid, precision=highest
    ) - jnp.einsum("kn,...nm->...km", first_sin, imag_grid, precision=highest)
    section_imag = jnp.einsum(
        "kn,...nm->...km", first_cos, imag_grid, precision=highest
    ) + jnp.einsum("kn,...nm->...km", first_sin, real_grid, precision=highest)
    twist_cos, twist_sin = table(size_low, size_high, length, direction)
    twisted_real = section_real * twist_cos - section_imag * twist_sin
    twisted_imag = section_real * twist_sin + section_imag * twist_cos
    second_cos, second_sin = table(size_high, size_high, size_high, direction)
    final_real = jnp.einsum(
        "bm,...km->...bk", second_cos, twisted_real, precision=highest
    ) - jnp.einsum("bm,...km->...bk", second_sin, twisted_imag, precision=highest)
    final_imag = jnp.einsum(
        "bm,...km->...bk", second_cos, twisted_imag, precision=highest
    ) + jnp.einsum("bm,...km->...bk", second_sin, twisted_real, precision=highest)
    return (final_real.reshape(lead_shape + (length,)), final_imag.reshape(lead_shape + (length,)))


def on_device(echo, steer, offsets, taps, centers, halves):
    echo_piece = gather_interp(echo, offsets, taps)
    part_real = jnp.einsum(
        "pr,ap->ra", echo_piece[0], steer[0], preferred_element_type=jnp.float32
    ) - jnp.einsum("pr,ap->ra", echo_piece[1], steer[1], preferred_element_type=jnp.float32)
    part_imag = jnp.einsum(
        "pr,ap->ra", echo_piece[0], steer[1], preferred_element_type=jnp.float32
    ) + jnp.einsum("pr,ap->ra", echo_piece[1], steer[0], preferred_element_type=jnp.float32)
    partial_value = jnp.stack([part_real, part_imag])
    reduced = lax.psum_scatter(partial_value, "ping", scatter_dimension=1, tiled=True)
    lines_image = lax.all_to_all(reduced, "rng", split_axis=1, concat_axis=2, tiled=True)
    length = lines_image.shape[2]
    cells = jnp.arange(length, dtype=jnp.int32)
    distance = (cells[None, :] - centers[:, None]) % length
    distance = jnp.minimum(distance, (length - distance) % length)
    inside = (distance <= halves[:, None]).astype(jnp.float32)
    stacked_real = jnp.stack([lines_image[0], lines_image[0] * inside])
    stacked_imag = jnp.stack([lines_image[1], lines_image[1] * inside])
    spec_real, spec_imag = transform(stacked_real, stacked_imag, -1.0)
    window_real = spec_real[1]
    window_imag = spec_imag[1]
    next_real = jnp.roll(window_real, -1, axis=1)
    next_imag = jnp.roll(window_imag, -1, axis=1)
    cross_real = window_real * next_real + window_imag * next_imag
    cross_imag = window_real * next_imag - window_imag * next_real
    angle = 2.0 * math.pi / length * centers.astype(jnp.float32)
    numer_local = jnp.sum(
        cross_real * jnp.sin(angle)[:, None] + cross_imag * jnp.cos(angle)[:, None], axis=0
    )
    denom_local = jnp.sum(window_real * window_real + window_imag * window_imag, axis=0)
    numer, denom = total_over(numer_local, denom_local)
    slope = numer / (denom + epsilon)
    phase_error = (
        jnp.cumsum(slope)
        - slope
        - jnp.arange(length, dtype=jnp.float32) * (jnp.sum(slope) / length)
    )
    cos_phase = jnp.cos(phase_error)[None, :]
    sin_phase = jnp.sin(phase_error)[None, :]
    full_real = spec_real[0]
    full_imag = spec_imag[0]
    fixed_real = full_real * cos_phase + full_imag * sin_phase
    fixed_imag = full_imag * cos_phase - full_real * sin_phase
    out_real, out_imag = transform(fixed_real, fixed_imag, 1.0)
    focused = jnp.stack([out_real, out_imag]) / length
    return (focused, phase_error)


def solution(mesh):
    in_specs = (
        P(None, ("leg", "ping"), "rng"),
        P(None, ("leg", "rng"), "ping"),
        P(("leg", "ping")),
        P(("leg", "ping"), None),
        P(("leg", "ping", "rng")),
        P(("leg", "ping", "rng")),
    )
    out_specs = (P(None, ("leg", "ping", "rng"), None), P("leg"))
    return jax.shard_map(
        on_device, mesh=mesh, in_specs=in_specs, out_specs=out_specs, check_vma=False
    )
```

profile of v0, /device:TPU:0, one launch (start us, length us, event | category | flops | bytes accessed | tf_op | source)
XLA Modules:
  0.0 247.2 jit_solution(1800306071366684526)
XLA Ops:
  9.7 18.5 %shard_map.77 = bf16[2,1024,256]{2,1,0:T(8,128)(2,1)S(1)} custom-call(s32[16]{0:T(128)S(1)} %copy-done.1, f32[16,4]{1,0:T(8,128)S(1)} %copy.24.taps_ref, bf16[2,1024,128]{2,1,0:T(8,128)(2,1)S(1)} %copy-done), custom_call_target="tpu_custom_call" | custom-call | tf_op jit(solution)/shard_map/pallas_call | solution.py:75
  28.1 5.8 %fusion.2 = f32[256,4096]{1,0:T(8,128)S(1)} fusion(bf16[2,4096,1024]{2,1,0:T(8,128)(2,1)} %param.7, bf16[2,1024,256]{2,1,0:T(8,128)(2,1)S(1)} %shard_map.77), kind=kOutput, calls=%fused_computation.3 | convolution fusion | flops 2147483648 | bytes 13107200 | tf_op jit(solution)/shard_map/pr,ap->ra/dot_general | solution.py:207
  33.9 5.8 %fusion = f32[256,4096]{1,0:T(8,128)S(1)} fusion(bf16[2,4096,1024]{2,1,0:T(8,128)(2,1)} %param.7, bf16[2,1024,256]{2,1,0:T(8,128)(2,1)S(1)} %shard_map.77), kind=kOutput, calls=%fused_computation.1 | convolution fusion | flops 2147483648 | bytes 13107200 | tf_op jit(solution)/shard_map/pr,ap->ra/dot_general | solution.py:208
  39.7 5.8 %fusion.15 = f32[1,256,4096]{2,1,0:T(8,128)S(1)} fusion(f32[256,4096]{1,0:T(8,128)S(1)} %fusion.2, bf16[2,4096,1024]{2,1,0:T(8,128)(2,1)} %param.7, bf16[2,1024,256]{2,1,0:T(8,128)(2,1)S(1)} %shard_map.77), kind=kOutput, calls=%fused_computation.14 | convolution fusion | flops 2148532224 | bytes 17301504 | tf_op jit(solution)/shard_map/pr,ap->ra/dot_general | solution.py:205
  45.5 5.8 %fusion.21 = f32[1,256,4096]{2,1,0:T(8,128)S(1)} fusion(f32[256,4096]{1,0:T(8,128)S(1)} %fusion, bf16[2,4096,1024]{2,1,0:T(8,128)(2,1)} %param.7, bf16[2,1024,256]{2,1,0:T(8,128)(2,1)S(1)} %shard_map.77), kind=kOutput, calls=%fused_computation.16 | convolution fusion | flops 2148532224 | bytes 17301504 | tf_op jit(solution)/shard_map/pr,ap->ra/dot_general | solution.py:210
  51.3 4.0 %pad_maximum_fusion = f32[2,256,4096]{2,1,0:T(8,128)} fusion(f32[1,256,4096]{2,1,0:T(8,128)S(1)} %fusion.21, f32[1,256,4096]{2,1,0:T(8,128)S(1)} %fusion.15), kind=kLoop, calls=%fused_computation | loop fusion | flops 2097152 | bytes 16777216 | tf_op jit(solution)/shard_map/stack | solution.py:211
  55.3 91.2 %reduce-scatter.2.cloned.1.call-done = f32[2,32,4096]{2,1,0:T(8,128)} async-done(((f32[2,256,4096]{2,1,0:T(8,128)}), f32[2,32,4096]{2,1,0:T(8,128)}) %reduce-scatter.2.cloned.1.call-update) | async-done | bytes 1048592 | tf_op jit(solution)/shard_map/reduce_scatter | solution.py:212
  146.5 3.0 %copy.25 = f32[2,32,4096]{2,0,1:T(2,128)} copy(f32[2,32,4096]{2,1,0:T(8,128)} %reduce-scatter.2.cloned.1.call-done) | data formatting | bytes 2097152 | tf_op jit(solution)/shard_map/reduce_scatter | solution.py:212
  149.5 3.8 %all-to-all-start = ((f32[2,32,4096]{2,0,1:T(2,128)}), f32[2,32,4096]{2,0,1:T(2,128)S(1)}, u32[]{:S(2)}, u32[]{:S(2)}) async-start(f32[2,32,4096]{2,0,1:T(2,128)} %copy.25), calls=%async_computation.1 | async-start | bytes 2097152 | tf_op jit(solution)/shard_map/all_to_all | solution.py:213
  153.7 11.6 %all-to-all-done = f32[2,32,4096]{2,0,1:T(2,128)S(1)} async-done(((f32[2,32,4096]{2,0,1:T(2,128)}), f32[2,32,4096]{2,0,1:T(2,128)S(1)}, u32[]{:S(2)}, u32[]{:S(2)}) %all-to-all-start) | async-done | bytes 1048608 | tf_op jit(solution)/shard_map/all_to_all | solution.py:213
  167.8 1.2 fusion.33
  168.9 1.2 fusion.32
  170.1 1.2 fusion.27
  171.3 1.2 fusion.26
  172.4 1.2 fusion.48
  173.7 1.2 fusion.24
  175.8 2.4 copy.30
  178.1 2.4 squeeze.38
  180.5 2.1 slice.96
  182.6 10.9 %fusion.47 = f32[2,16,64,128]{3,2,1,0:T(8,128)S(1)} fusion(f32[2,16,64,128]{3,2,1,0:T(8,128)S(1)} %fusion.26, f32[2,16,64,128]{3,2,1,0:T(8,128)S(1)} %fusion.27, f32[64,128]{1,0:T(8,128)S(1)} %get-tuple-element.16, f32[64,128]{1,0:T(8,128)S(1)} %get-tuple-element.17), kind=kOutput, calls=%fused_computation.70 | convolution fusion | flops 403668992 | bytes 3211264 | tf_op jit(solution)/shard_map/bm,...km->...bk/dot_general | solution.py:194
  193.5 1.2 fusion.25
  196.6 1.5 copy.28
  198.0 1.2 squeeze.37
  199.2 2.0 slice.93
  201.9 1.9 pad_maximum_fusion.8
  203.9 1.5 concatenate.24
  205.3 1.1 copy.31
  206.5 1.9 pad_maximum_fusion.7
  208.4 1.5 concatenate.22
  211.0 1.6 add_reduce_fusion.1
  213.5 13.1 %shard_map.78 = f32[16,8,128]{2,1,0:T(8,128)} custom-call(f32[16,8,128]{2,1,0:T(8,128)} %pad_maximum_fusion.9.value_ref), custom_call_target="tpu_custom_call" | custom-call | tf_op jit(solution)/shard_map/pallas_call | solution.py:139
  226.6 1.4 fusion.189
  (58 shorter events, 22.1 us)
Async XLA Ops:
  7.2 139.4 %reduce-scatter.2.cloned.1.call-start = ((), (), s32[]{:S(2)}) async-start(), calls=%async_computation.2 | async-start | bytes 9437184 | tf_op jit(solution)/shard_map/reduce_scatter | solution.py:212
  8.0 1.0 copy-start
  9.0 0.7 copy-start.1
  55.3 98.4 %copy-start.5 = (s32[16]{0:T(128)S(1)}, s32[16]{0:T(128)}, u32[]{:S(2)}) copy-start(s32[16]{0:T(128)} %param.10) | copy-start | bytes 196
  55.3 111.9 %copy-start.4 = (s32[16]{0:T(128)S(1)}, s32[16]{0:T(128)}, u32[]{:S(2)}) copy-start(s32[16]{0:T(128)} %param.11) | copy-start | bytes 196
  149.5 15.8 %all-to-all-start = ((f32[2,32,4096]{2,0,1:T(2,128)}), f32[2,32,4096]{2,0,1:T(2,128)S(1)}, u32[]{:S(2)}, u32[]{:S(2)}) async-start(f32[2,32,4096]{2,0,1:T(2,128)} %copy.25), calls=%async_computation.1 | async-start | bytes 2097152 | tf_op jit(solution)/shard_map/all_to_all | solution.py:213
  180.5 21.4 %slice-start = ((f32[16,8192]{1,0:T(8,128)}), f32[16,1]{1,0:T(8,128)S(1)}, s32[]{:S(2)}) async-start(f32[16,8192]{1,0:T(8,128)} %squeeze.38), calls=%async_computation.3 | async-start | bytes 16384 | tf_op jit(solution)/shard_map/jit(_roll_static)/slice | solution.py:225
  194.8 1.0 copy-start.2
  196.6 14.4 %copy-start.3 = (f32[2,16,128,64]{2,3,1,0:T(8,128)S(1)}, f32[2,16,128,64]{2,3,1,0:T(8,128)}, u32[]{:S(2)}) copy-start(f32[2,16,128,64]{2,3,1,0:T(8,128)} %copy-done.2) | copy-start | bytes 3145732
Sparse Core Ops, SparseCore 0:
  55.5 91.0 reduce-scatter.1
where the time goes:
time: 252 us; the launch traced here: 247 us
  waiting for transfers between devices  103 us (41%)
  matrix products  48.8 us (19%)
  Pallas kernels  31.5 us (12%)
  local copies, waits for them, and re-layouts  30.3 us (12%)
  between operations  15.2 us (6%)
  other arithmetic  14.7 us (6%)
  starting transfers between devices  3.88 us (2%)
    reduce_scatter x1, waiting for transfers between devices, on_device(): lax.psum_scatter(partial_value, 'ping', scatter_dimension=1, tiled=True)  91.2 us
    pallas_call x1, Pallas kernels, gather_interp(): pl.pallas_call(functools.partial(interp_kernel, tiles), out_shape=jax.Sha...  18.5 us
    pallas_call x1, Pallas kernels, total_over(): pl.pallas_call(functools.partial(total_kernel, pings, tiles), out_shape=j...  13.1 us
    dot_general x2, matrix products, transform(): jnp.einsum('bm,...km->...bk', second_cos, twisted_real, precision=highest)  11.7 us
    all_to_all x1, waiting for transfers between devices, on_device(): lax.all_to_all(reduced, 'rng', split_axis=1, concat_axis=2, tiled=True)  11.6 us
    dot_general x1, matrix products, on_device(): jnp.einsum('pr,ap->ra', echo_piece[1], steer[0], preferred_element_type=j...  5.78 us
    dot_general x1, matrix products, on_device(): jnp.einsum('pr,ap->ra', echo_piece[0], steer[0], preferred_element_type=j...  5.77 us
    dot_general x1, matrix products, on_device(): jnp.einsum('pr,ap->ra', echo_piece[1], steer[1], preferred_element_type=j...  5.77 us
  transfers between devices with their start and end apart: 2, of which 2 were waited for; matrix products, arithmetic and copies ran while one was open for 0% of the time, Pallas kernels for 0%

commit v1 on v0

--- a/solution.py
+++ b/solution.py
@@ -18,28 +18,94 @@
 MESH = pl.DeviceIdType.MESH
 
 
-def meet(peers):
+CORES = 2
+LAG = 2
+
+
+def meet(peers, extra):
     barrier = pltpu.get_barrier_semaphore()
     for peer in peers:
         pl.semaphore_signal(barrier, inc=1, device_id=peer, device_id_type=MESH)
-    pl.semaphore_wait(barrier, len(peers))
-
-
-def interp_kernel(tiles, offsets_ref, taps_ref, echo_ref, out_ref, held, send_sem, recv_sem, own_sem):
+    total = len(peers)
+    for present, peer in extra:
+        total = total + present.astype(jnp.int32)
+
+        @pl.when(present)
+        def _():
+            pl.semaphore_signal(barrier, inc=1, device_id=peer, device_id_type=MESH)
+
+    pl.semaphore_wait(barrier, total)
+
+
+def encode(value, target):
+    count, width = value.shape
+    groups = count // 16
+    peak = jnp.max(jnp.abs(value), axis=1, keepdims=True)
+    power = jnp.floor(jnp.log2(jnp.maximum(peak, 1e-30)) + 1.01)
+    whole = jnp.round(value * jnp.exp2(15.0 - power)).astype(jnp.int32).astype(jnp.int16)
+    for piece in range(width // 128):
+        target[piece * count:(piece + 1) * count, :] = whole[:, piece * 128:(piece + 1) * 128]
+    lane = lax.broadcasted_iota(jnp.int32, (16, 128), 1) // (128 // groups)
+    powers = jnp.zeros((16, 128), jnp.float32)
+    for group in range(groups):
+        powers = jnp.where(lane == group, power[group * 16:(group + 1) * 16], powers)
+    target[width // 128 * count:, :] = powers.astype(jnp.int32).astype(jnp.int16)
+
+
+def decode(source, count, width):
+    groups = count // 16
+    powers = source[width // 128 * count:, :].astype(jnp.int32).astype(jnp.float32)
+    scales = jnp.exp2(powers - 15.0)
+    span = 128 // groups
+    scale = jnp.concatenate(
+        [scales[:, group * span:group * span + 1] for group in range(groups)], axis=0
+    )
+    pieces = [
+        source[piece * count:(piece + 1) * count, :].astype(jnp.int32).astype(jnp.float32) * scale
+        for piece in range(width // 128)
+    ]
+    return jnp.concatenate(pieces, axis=1)
+
+
+def image_kernel(
+    plan, offsets_ref, taps_ref, echo_ref, steer_ref, out_ref,
+    held, left, weights, part, got, away, near, fin, side,
+    own_sem, echo_send, echo_recv, load_sem, pair_send, pair_recv,
+    line_send, line_recv, side_send, side_recv,
+):
+    tiles, chips, chunks, width, lines = plan
+    pings = echo_ref.shape[1]
+    columns = echo_ref.shape[2]
+    count = tiles * 2 * lines
     me = lax.axis_index("rng")
-    columns = echo_ref.shape[2]
-    width = tiles * columns
+    chip = lax.axis_index("ping") // CORES
+    core = lax.axis_index("ping") % CORES
+    last = chips - 1
+
+    def load(chunk, half):
+        return pltpu.make_async_copy(
+            steer_ref.at[half, pl.ds(chunk * width, width), :],
+            weights.at[chunk, :, pl.ds(half * pings, pings)],
+            load_sem.at[chunk, half],
+        )
+
+    for chunk in range(chunks):
+        for half in range(2):
+            load(chunk, half).start()
     own = pltpu.make_async_copy(echo_ref, held.at[me], own_sem)
     own.start()
     peers = [{"rng": lax.rem(me + step, tiles)} for step in range(1, tiles)]
-    meet(peers)
+    partner = {"ping": chip * CORES + 1 - core}
+    above = {"ping": (chip + 1) * CORES + core}
+    below = {"ping": (chip - 1) * CORES + core}
+    meet(peers + [partner], [(chip < last, above), (chip > 0, below)])
     copies = []
     for step, peer in enumerate(peers):
         copy = pltpu.make_async_remote_copy(
             src_ref=echo_ref,
             dst_ref=held.at[me],
-            send_sem=send_sem.at[step],
-            recv_sem=recv_sem.at[step],
+            send_sem=echo_send.at[step],
+            recv_sem=echo_recv.at[step],
             device_id=peer,
             device_id_type=MESH,
         )
@@ -49,44 +115,239 @@
     for copy in copies:
         copy.wait()
 
-    def block(index, carry):
-        rows = pl.ds(pl.multiple_of(index * PBLK, PBLK), PBLK)
-        offset = offsets_ref[index]
-        for part in range(2):
-            value = jnp.concatenate([held[tile, part, rows, :] for tile in range(tiles)], axis=1)
-            value = value.astype(jnp.float32)
-            column = lax.broadcasted_iota(jnp.int32, (PBLK, width), 1)
-            result = jnp.zeros((PBLK, width), jnp.float32)
-            for tap in range(NTAP):
-                shift = offset + tap
-                moved = jnp.where(column >= shift, pltpu.roll(value, shift, axis=1), 0.0)
-                result = result + taps_ref[index, tap] * moved
-            out_ref[part, rows, :] = result.astype(jnp.bfloat16)
+    full = tiles * columns
+    column = lax.broadcasted_iota(jnp.int32, (PBLK, full), 1)
+
+    def interpolate(index, carry):
+        cols = pl.multiple_of(index * 128, 128)
+        turned = []
+        for half in range(2):
+            blocks = []
+            for inner in range(128 // PBLK):
+                block = index * (128 // PBLK) + inner
+                rows = pl.ds(pl.multiple_of(block * PBLK, PBLK), PBLK)
+                value = jnp.concatenate([held[tile, half, rows, :] for tile in range(tiles)], axis=1)
+                value = value.astype(jnp.float32)
+                offset = offsets_ref[block]
+                result = jnp.zeros((PBLK, full), jnp.float32)
+                for tap in range(NTAP):
+                    shift = offset + tap
+                    moved = jnp.where(column >= shift, pltpu.roll(value, shift, axis=1), 0.0)
+                    result = result + taps_ref[block, tap] * moved
+                blocks.append(result)
+            turned.append(jnp.concatenate(blocks, axis=0).T)
+        real, imag = turned
+        for parity in range(CORES):
+            for target in range(chips):
+                for tile in range(tiles):
+                    first = ((target * CORES + parity) * tiles + tile) * lines
+                    place = ((parity * chips + target) * tiles + tile) * 2 * lines
+                    a = real[first:first + lines].astype(jnp.bfloat16)
+                    b = imag[first:first + lines].astype(jnp.bfloat16)
+                    left[place:place + lines, pl.ds(cols, 128)] = a
+                    left[place + lines:place + 2 * lines, pl.ds(cols, 128)] = b
+                    left[place:place + lines, pl.ds(pings + cols, 128)] = -b
+                    left[place + lines:place + 2 * lines, pl.ds(pings + cols, 128)] = a
         return carry
 
-    lax.fori_loop(0, out_ref.shape[1] // PBLK, block, 0)
-
-
-def gather_interp(echo, offsets, taps):
+    lax.fori_loop(0, pings // 128, interpolate, 0)
+
+    def pair(chunk):
+        return pltpu.make_async_remote_copy(
+            src_ref=part.at[chunk, 1 - core],
+            dst_ref=got.at[chunk],
+            send_sem=pair_send.at[chunk],
+            recv_sem=pair_recv.at[chunk],
+            device_id=partner,
+            device_id_type=MESH,
+        )
+
+    def line(way, target, chunk):
+        return pltpu.make_async_remote_copy(
+            src_ref=away.at[way, target, chunk],
+            dst_ref=near.at[way, target, chunk],
+            send_sem=line_send.at[way, target, chunk],
+            recv_sem=line_recv.at[way, target, chunk],
+            device_id=(above, below)[way],
+            device_id_type=MESH,
+        )
+
+    def collect(way, target, chunk):
+        line(way, target, chunk).wait_recv()
+        rows = pl.ds(pl.multiple_of(target * count, count), count)
+        part[chunk, core, rows, :] += decode(near.at[way, target, chunk], count, width)
+
+    def pass_on(way, target, chunk, first):
+        @pl.when(jnp.logical_not(first))
+        def _():
+            collect(way, target, chunk)
+
+        encode(part[chunk, core, target * count:(target + 1) * count, :], away.at[way, target, chunk])
+        line(way, target, chunk).start()
+
+    block = min(512, CORES * chips * count)
+    halves = chips * count
+
+    def multiply(chunk):
+        for half in range(2):
+            load(chunk, half).wait()
+
+        def rows_of(index, carry):
+            rows = pl.ds(pl.multiple_of(index * block, block), block)
+            value = lax.dot_general(
+                left[rows, :], weights[chunk], (((1,), (1,)), ((), ())),
+                preferred_element_type=jnp.float32,
+            )
+            if block > halves:
+                part[chunk, 0] = value[:halves]
+                part[chunk, 1] = value[halves:]
+            else:
+                inside = pl.ds(pl.multiple_of(index % (halves // block) * block, block), block)
+                part[chunk, index // (halves // block), inside, :] = value
+            return carry
+
+        lax.fori_loop(0, CORES * halves // block, rows_of, 0)
+        pair(chunk).start()
+
+    def step(time, carry):
+        @pl.when(time < chunks)
+        def _():
+            multiply(time)
+
+        chunk = time - 1
+
+        @pl.when(jnp.logical_and(chunk >= 0, chunk < chunks))
+        def _():
+            pair(chunk).wait_recv()
+            part[chunk, core] += got[chunk]
+
+        for way in range(2):
+            hops = (chip, last - chip)[way]
+            at = chunk - hops * LAG
+            ready = jnp.logical_and(at >= 0, at < chunks)
+            for away_by in range(chips - 2):
+                target = (last - away_by, away_by)[way]
+                ahead = (chip < target, chip > target)[way]
+
+                @pl.when(jnp.logical_and(ready, ahead))
+                def _():
+                    pass_on(way, target, at, hops == 0)
+
+        return carry
+
+    lax.fori_loop(0, chunks + 1 + (chips - 1) * LAG, step, 0)
+
+    def nearest(chunk, carry):
+        @pl.when(chip == 0)
+        def _():
+            pass_on(0, 1, chunk, True)
+
+        @pl.when(chip == last)
+        def _():
+            pass_on(1, last - 1, chunk, True)
+
+        return carry
+
+    lax.fori_loop(0, chunks, nearest, 0)
+
+    def across(step, chunk):
+        peer = lax.rem(me + step, tiles)
+        return pltpu.make_async_remote_copy(
+            src_ref=fin.at[chunk, peer],
+            dst_ref=side.at[chunk, step - 1],
+            send_sem=side_send.at[step - 1, chunk],
+            recv_sem=side_recv.at[step - 1, chunk],
+            device_id={"rng": peer},
+            device_id_type=MESH,
+        )
+
+    def place(source, chunk, value):
+        start = pl.multiple_of(source * (chunks * width) + chunk * width, width)
+        out_ref[0, :, pl.ds(start, width)] = value[:lines]
+        out_ref[1, :, pl.ds(start, width)] = value[lines:]
+
+    def finish(chunk, carry):
+        @pl.when(chip > 0)
+        def _():
+            collect(0, chip, chunk)
+
+        @pl.when(chip < last)
+        def _():
+            collect(1, chip, chunk)
+
+        for tile in range(tiles):
+            rows = pl.ds(pl.multiple_of(chip * count + tile * 2 * lines, 2 * lines), 2 * lines)
+            fin[chunk, tile] = part[chunk, core, rows, :]
+        for step in range(1, tiles):
+            across(step, chunk).start()
+        place(me, chunk, fin[chunk, me])
+        return carry
+
+    lax.fori_loop(0, chunks, finish, 0)
+
+    def arrive(chunk, carry):
+        for step in range(1, tiles):
+            across(step, chunk).wait()
+            place(lax.rem(me + tiles - step, tiles), chunk, side[chunk, step - 1])
+        pair(chunk).wait_send()
+        for way in range(2):
+            for target in range(chips):
+                ahead = (chip < target, chip > target)[way]
+
+                @pl.when(ahead)
+                def _():
+                    line(way, target, chunk).wait_send()
+
+        return carry
+
+    lax.fori_loop(0, chunks, arrive, 0)
+
+
+def lines_image(echo, steer, offsets, taps):
     tiles = lax.axis_size("rng")
-    rows, columns = echo.shape[1:]
+    chips = lax.axis_size("ping") // CORES
+    pings, columns = echo.shape[1:]
+    cells = steer.shape[1]
+    width = 512 if cells % 4096 == 0 else 256
+    chunks = cells // width
+    lines = columns // (chips * CORES)
+    count = tiles * 2 * lines
+    rows = chips * count
     vmem = pl.BlockSpec(memory_space=pltpu.VMEM)
     smem = pl.BlockSpec(memory_space=pltpu.SMEM)
+    dma = pltpu.SemaphoreType.DMA
+    message = (width // 128 * count + 16, 128)
+    others = max(tiles - 1, 1)
     return pl.pallas_call(
-        functools.partial(interp_kernel, tiles),
-        out_shape=jax.ShapeDtypeStruct((2, rows, tiles * columns), jnp.bfloat16),
-        in_specs=[smem, smem, vmem],
+        functools.partial(image_kernel, (tiles, chips, chunks, width, lines)),
+        out_shape=jax.ShapeDtypeStruct((2, lines, tiles * cells), jnp.float32),
+        in_specs=[smem, smem, vmem, pl.BlockSpec(memory_space=pl.ANY)],
         out_specs=vmem,
         scratch_shapes=[
-            pltpu.VMEM((tiles, 2, rows, columns), jnp.bfloat16),
-            pltpu.SemaphoreType.DMA((tiles - 1,)),
-            pltpu.SemaphoreType.DMA((tiles - 1,)),
-            pltpu.SemaphoreType.DMA,
+            pltpu.VMEM((tiles, 2, pings, columns), jnp.bfloat16),
+            pltpu.VMEM((CORES * rows, 2 * pings), jnp.bfloat16),
+            pltpu.VMEM((chunks, width, 2 * pings), jnp.bfloat16),
+            pltpu.VMEM((chunks, CORES, rows, width), jnp.float32),
+            pltpu.VMEM((chunks, rows, width), jnp.float32),
+            pltpu.VMEM((2, chips, chunks) + message, jnp.int16),
+            pltpu.VMEM((2, chips, chunks) + message, jnp.int16),
+            pltpu.VMEM((chunks, tiles, 2 * lines, width), jnp.float32),
+            pltpu.VMEM((chunks, others, 2 * lines, width), jnp.float32),
+            dma,
+            dma((others,)),
+            dma((others,)),
+            dma((chunks, 2)),
+            dma((chunks,)),
+            dma((chunks,)),
+            dma((2, chips, chunks)),
+            dma((2, chips, chunks)),
+            dma((others, chunks)),
+            dma((others, chunks)),
         ],
         compiler_params=pltpu.CompilerParams(
-            collective_id=0, has_side_effects=True, vmem_limit_bytes=48 * 2**20
+            collective_id=0, has_side_effects=True, vmem_limit_bytes=60 * 2**20
         ),
-    )(offsets, taps, echo)
+    )(offsets, taps, echo, steer)
 
 
 def total_kernel(pings, tiles, value_ref, out_ref, held, full, send_sem, recv_sem, send_two, recv_two):
@@ -94,7 +355,7 @@
     me = lax.axis_index("ping") * tiles + lax.axis_index("rng")
     ids = [lax.rem(me + step, count) for step in range(1, count)]
     peers = [{"ping": lax.div(one, tiles), "rng": lax.rem(one, tiles)} for one in ids]
-    meet(peers)
+    meet(peers, [])
     copies = []
     for step, peer in enumerate(peers):
         copy = pltpu.make_async_remote_copy(
@@ -201,23 +462,14 @@
 
 
 def on_device(echo, steer, offsets, taps, centers, halves):
-    echo_piece = gather_interp(echo, offsets, taps)
-    part_real = jnp.einsum(
-        "pr,ap->ra", echo_piece[0], steer[0], preferred_element_type=jnp.float32
-    ) - jnp.einsum("pr,ap->ra", echo_piece[1], steer[1], preferred_element_type=jnp.float32)
-    part_imag = jnp.einsum(
-        "pr,ap->ra", echo_piece[0], steer[1], preferred_element_type=jnp.float32
-    ) + jnp.einsum("pr,ap->ra", echo_piece[1], steer[0], preferred_element_type=jnp.float32)
-    partial_value = jnp.stack([part_real, part_imag])
-    reduced = lax.psum_scatter(partial_value, "ping", scatter_dimension=1, tiled=True)
-    lines_image = lax.all_to_all(reduced, "rng", split_axis=1, concat_axis=2, tiled=True)
-    length = lines_image.shape[2]
+    image = lines_image(echo, steer, offsets, taps)
+    length = image.shape[2]
     cells = jnp.arange(length, dtype=jnp.int32)
     distance = (cells[None, :] - centers[:, None]) % length
     distance = jnp.minimum(distance, (length - distance) % length)
     inside = (distance <= halves[:, None]).astype(jnp.float32)
-    stacked_real = jnp.stack([lines_image[0], lines_image[0] * inside])
-    stacked_imag = jnp.stack([lines_image[1], lines_image[1] * inside])
+    stacked_real = jnp.stack([image[0], image[0] * inside])
+    stacked_imag = jnp.stack([image[1], image[1] * inside])
     spec_real, spec_imag = transform(stacked_real, stacked_imag, -1.0)
     window_real = spec_real[1]
     window_imag = spec_imag[1]

time: 252 us -> 129 us (0.51); the launches traced: 247 us -> 128 us
  waiting for transfers between devices: 103 us -> 0 us
  Pallas kernels: 31.5 us -> 81.6 us
  matrix products: 48.8 us -> 16.2 us
  between operations: 15.2 us -> 1.67 us
  local copies, waits for them, and re-layouts: 30.3 us -> 19.8 us
  other arithmetic: 14.7 us -> 9.1 us
  starting transfers between devices: 3.88 us -> 0 us
    reduce_scatter x1 -> x0, waiting for transfers between devices: 91.2 us -> none  [on_device(): lax.psum_scatter(partial_value, 'ping', scatter_dimension=1, tiled=True)]
    pallas_call x1, Pallas kernels: 18.5 us -> 63.7 us  [lines_image(): pl.pallas_call(functools.partial(image_kernel, (tiles, chips, chunks, wid...]
    dot_general x4 -> x0, matrix products: 23.1 us -> none  [the longest x1 5.78 us: on_device(): jnp.einsum('pr,ap->ra', echo_piece[1], steer[0], preferred_element_type=j...]
    all_to_all x1 -> x0, waiting for transfers between devices: 11.6 us -> none  [on_device(): lax.all_to_all(reduced, 'rng', split_axis=1, concat_axis=2, tiled=True)]
    dot_general x2, matrix products: 11.7 us -> 2.05 us  [transform(): jnp.einsum('bm,...km->...bk', second_cos, twisted_real, precision=highest)]
    pallas_call x1, Pallas kernels: 13.1 us -> 17.9 us  [total_over(): pl.pallas_call(functools.partial(total_kernel, pings, tiles), out_shape=j...]
    another operation x3 -> x2, other arithmetic: 4.42 us -> 0.39 us  [the longest x1 4.04 us: on_device(): partial_value = jnp.stack([part_real, part_imag])]
    all_to_all x1 -> x0, starting transfers between devices: 3.84 us -> none  [on_device(): lax.all_to_all(reduced, 'rng', split_axis=1, concat_axis=2, tiled=True)]
  transfers between devices with their start and end apart: 2 -> 0, of which waited for: 2 -> 0; matrix products, arithmetic and copies ran while one was open for 0% -> 0% of each run, Pallas kernels for 0% -> 0%
where the time goes in v1:
time: 129 us; the launch traced here: 128 us
  Pallas kernels  81.6 us (63%)
  local copies, waits for them, and re-layouts  19.8 us (15%)
  matrix products  16.2 us (13%)
  other arithmetic  9.1 us (7%)
  between operations  1.67 us (1%)
    pallas_call x1, Pallas kernels, lines_image(): pl.pallas_call(functools.partial(image_kernel, (tiles, chips, chunks, wid...  63.7 us
    pallas_call x1, Pallas kernels, total_over(): pl.pallas_call(functools.partial(total_kernel, pings, tiles), out_shape=j...  17.9 us
    concatenate x2, local copies, waits for them, and re-layouts, on_device(): next_imag = jnp.roll(window_imag, -1, axis=1)  4.77 us
    slice x2, local copies, waits for them, and re-layouts, on_device(): window_imag = spec_imag[1]  3.18 us
    unnamed x13, local copies, waits for them, and re-layouts  2.82 us

profile of v1, /device:TPU:0, one launch (start us, length us, event | category | flops | bytes accessed | tf_op | source)
XLA Modules:
  0.0 128.4 jit_solution(15017773229818008826)
XLA Ops:
  0.7 1.4 %copy.20.taps_ref = f32[16,4]{1,0:T(8,128)} copy(f32[16,4]{0,1:T(4,128)} %param.9) | data formatting | bytes 512 | tf_op args[3]
  2.0 63.7 %shard_map.77 = f32[2,16,8192]{2,1,0:T(8,128)} custom-call(s32[16]{0:T(128)} %offsets_ref.1, f32[16,4]{1,0:T(8,128)} %copy.20.taps_ref, bf16[2,1024,128]{2,1,0:T(8,128)(2,1)} %echo_ref.1, bf16[2,4096,1024]{2,1,0:T(8,128)(2,1)} %steer_ref.1), custom_call_target="tpu_custom_call" | custom-call | tf_op jit(solution)/shard_map/pallas_call | solution.py:321
  65.7 1.8 %select_bitcast_fusion.1 = (f32[2,8,64,128]{3,1,2,0:T(8,128)S(1)}, f32[2,8,64,128]{3,1,2,0:T(8,128)S(1)}, f32[2,8,64,128]{3,1,2,0:T(8,128)S(1)}, f32[2,8,64,128]{3,1,2,0:T(8,128)S(1)}) fusion(f32[2,16,8192]{2,1,0:T(8,128)} %shard_map.77, s32[16]{0:T(128)S(1)} %copy-done.1, s32[16]{0:T(128)S(1)} %copy-done.2), kind=kLoop, calls=%fused_computation.42 | loop fusion | flops 3670016 | bytes 3145856
  67.8 1.1 fusion.48
  69.3 1.2 fusion.3
  70.5 1.2 fusion.46
  71.6 1.2 fusion.2
  73.0 1.2 fusion.17
  74.2 1.2 fusion
  75.5 0.8 slice.71
  76.3 2.4 %copy.24 = f32[1,16,128,64]{3,2,1,0:T(8,128)} copy(f32[1,16,128,64]{2,3,1,0:T(8,128)} %slice.71) | data formatting | bytes 1048576 | tf_op jit(solution)/shard_map/slice | solution.py:475
  78.6 2.4 %squeeze.18 = f32[16,8192]{1,0:T(8,128)} reshape(f32[1,16,128,64]{3,2,1,0:T(8,128)} %copy.24) | data formatting | bytes 1048576 | tf_op jit(solution)/shard_map/squeeze | solution.py:475
  81.0 1.2 slice.72
  82.2 0.7 slice.73
  82.9 0.9 pad_maximum_fusion.1
  83.8 2.4 %concatenate.24 = f32[1,16,128,64]{3,2,1,0:T(8,128)} reshape(f32[16,8192]{1,0:T(8,128)} %pad_maximum_fusion.1) | data formatting | bytes 1048576 | tf_op jit(solution)/shard_map/jit(_roll_static)/concatenate | solution.py:477
  86.2 2.3 %copy.25 = f32[1,16,128,64]{2,3,1,0:T(8,128)} copy(f32[1,16,128,64]{3,2,1,0:T(8,128)} %concatenate.24) | data formatting | bytes 1048576 | tf_op jit(solution)/shard_map/jit(_roll_static)/concatenate | solution.py:477
  88.6 1.2 fusion.16
  89.8 1.4 %fusion.1 = f32[2,16,128,64]{2,3,1,0:T(8,128)S(1)} fusion(f32[2,16,64,128]{3,2,1,0:T(8,128)S(1)} %fusion.16, f32[2,16,64,128]{3,2,1,0:T(8,128)S(1)} %fusion.2, f32[2,16,64,128]{3,2,1,0:T(8,128)S(1)} %fusion.3, f32[64,128]{1,0:T(8,128)S(1)} %get-tuple-element.16, f32[64,128]{1,0:T(8,128)S(1)} %get-tuple-element.17), kind=kOutput, calls=%fused_computation.3 | convolution fusion | flops 403931136 | bytes 4259840 | tf_op jit(solution)/shard_map/bm,...km->...bk/dot_general | solution.py:457
  91.3 1.0 copy-done
  94.1 1.7 %add_reduce_fusion.1 = (f32[128,64]{0,1:T(8,128)S(1)}, f32[128,64]{0,1:T(8,128)S(1)}, f32[1,16,128,64]{2,3,1,0:T(8,128)S(1)}, f32[1,16,128,64]{2,3,1,0:T(8,128)S(1)}) fusion(f32[1,16,128,64]{2,3,1,0:T(8,128)S(1)} %copy.23, f32[1,16,128,64]{2,3,1,0:T(8,128)} %copy.25, f32[16]{0:T(128)S(1)} %get-tuple-element.15, f32[16]{0:T(128)S(1)} %get-tuple-element.14, ...), kind=kLoop, calls=%fused_computation.40 | loop fusion | flops 1818624 | bytes 4259968 | tf_op jit(solution)/shard_map/reduce_sum | solution.py:481
  96.7 17.9 %shard_map.78 = f32[16,8,128]{2,1,0:T(8,128)} custom-call(f32[16,8,128]{2,1,0:T(8,128)} %pad_maximum_fusion.2.value_ref), custom_call_target="tpu_custom_call" | custom-call | tf_op jit(solution)/shard_map/pallas_call | solution.py:400
  114.6 1.4 %fusion.156 = (f32[]{:T(128)}, f32[8,8,128]{2,1,0:T(8,128)S(1)}) fusion(f32[16,8,128]{2,1,0:T(8,128)} %shard_map.78), kind=kLoop, calls=%fused_computation.200 | loop fusion | flops 24575 | bytes 98308 | tf_op jit(solution)/shard_map/reduce_sum | solution.py:490
  119.3 0.8 fusion.18
  120.1 0.8 fusion.7
  120.9 0.8 fusion.19
  121.7 0.8 fusion.6
  122.6 0.8 fusion.20
  123.4 0.8 fusion.5
  125.0 0.8 fusion.21
  125.8 0.8 fusion.4
  127.3 1.0 maximum_multiply_fusion
  (43 shorter events, 7.6 us)
Async XLA Ops:
  0.6 65.1 %copy-start.2 = (s32[16]{0:T(128)S(1)}, s32[16]{0:T(128)}, u32[]{:S(2)}) copy-start(s32[16]{0:T(128)} %param.10) | copy-start | bytes 196
  0.6 65.1 %copy-start.1 = (s32[16]{0:T(128)S(1)}, s32[16]{0:T(128)}, u32[]{:S(2)}) copy-start(s32[16]{0:T(128)} %param.11) | copy-start | bytes 196
  91.3 1.0 copy-start

commit v2 on v1

--- a/solution.py
+++ b/solution.py
@@ -3,6 +3,7 @@
 
 import jax
 import jax.numpy as jnp
+import numpy as np
 from jax import lax
 from jax.experimental import pallas as pl
 from jax.experimental.pallas import tpu as pltpu
@@ -350,16 +351,126 @@
     )(offsets, taps, echo, steer)
 
 
-def total_kernel(pings, tiles, value_ref, out_ref, held, full, send_sem, recv_sem, send_two, recv_two):
-    count = pings * tiles
+LANES = 128
+
+
+def split(value):
+    high = value.astype(jnp.bfloat16)
+    return high, (value - high.astype(jnp.float32)).astype(jnp.bfloat16)
+
+
+def exact_dot(left, right):
+    total = None
+    for _ in range(3):
+        piece = right.astype(jnp.bfloat16)
+        term = jnp.dot(left, piece, preferred_element_type=jnp.float32)
+        total = term if total is None else total + term
+        right = right - piece.astype(jnp.float32)
+    return total
+
+
+def dot_exact(left, right):
+    total = None
+    for _ in range(3):
+        piece = left.astype(jnp.bfloat16)
+        term = jnp.dot(piece, right, preferred_element_type=jnp.float32)
+        total = term if total is None else total + term
+        left = left - piece.astype(jnp.float32)
+    return total
+
+
+def focus_kernel(
+    count, tiles, centers_ref, halves_ref, down_ref, up_ref, over_ref, back_ref, twist_ref,
+    image_ref, out_ref, phase_ref,
+    grid, spec, value, held, full, turned, send_sem, recv_sem, send_two, recv_two,
+):
     me = lax.axis_index("ping") * tiles + lax.axis_index("rng")
     ids = [lax.rem(me + step, count) for step in range(1, count)]
     peers = [{"ping": lax.div(one, tiles), "rng": lax.rem(one, tiles)} for one in ids]
-    meet(peers, [])
+    barrier = pltpu.get_barrier_semaphore()
+    for peer in peers:
+        pl.semaphore_signal(barrier, inc=1, device_id=peer, device_id_type=MESH)
+
+    lines, length = image_ref.shape[1:]
+    high = length // LANES
+    for half in range(2):
+        for row in range(high):
+            grid[pl.ds(half * high + row, lines, stride=2 * high), :] = image_ref[
+                half, :, row * LANES:(row + 1) * LANES
+            ]
+
+    cells = lax.broadcasted_iota(jnp.int32, (high, LANES), 0) * LANES
+    cells = cells + lax.broadcasted_iota(jnp.int32, (high, LANES), 1)
+    bottom = lax.broadcasted_iota(jnp.int32, (8, LANES), 0) == 7
+    lane = lax.broadcasted_iota(jnp.int32, (8, LANES), 1)
+    angle = jnp.zeros((8, LANES), jnp.float32)
+    for line in range(lines):
+        angle = jnp.where(lane == line, centers_ref[line].astype(jnp.float32), angle)
+    angle = angle * (2.0 * math.pi / length)
+    turned[0] = jnp.cos(angle)
+    turned[1] = jnp.sin(angle)
+
+    def after(part):
+        moved = pltpu.roll(part, high - 1, axis=0)
+        end = moved[high - 8:]
+        end = jnp.where(bottom, pltpu.roll(end, LANES - 1, axis=1), end)
+        return jnp.concatenate([moved[:high - 8], end], axis=0)
+
+    def forward(line, carry):
+        numer, denom = carry
+        rows = pl.ds(pl.multiple_of(line * 2 * high, 2 * high), 2 * high)
+        whole = grid[rows, :]
+        distance = cells - centers_ref[line]
+        distance = jnp.where(distance < 0, distance + length, distance)
+        distance = jnp.minimum(distance, length - distance)
+        inside = (distance <= halves_ref[line]).astype(jnp.float32)
+        chosen = whole * jnp.concatenate([inside, inside], axis=0)
+        top, low = split(jnp.concatenate([whole, chosen], axis=1))
+        first = jnp.dot(
+            down_ref[...], jnp.concatenate([top, low, top], axis=0), preferred_element_type=jnp.float32
+        )
+        pieces = []
+        for which in range(2):
+            real = first[:high, which * LANES:(which + 1) * LANES]
+            imag = first[high:, which * LANES:(which + 1) * LANES]
+            pieces.append(
+                jnp.concatenate(
+                    [
+                        real * twist_ref[0] + imag * twist_ref[1],
+                        imag * twist_ref[0] - real * twist_ref[1],
+                    ],
+                    axis=1,
+                )
+            )
+        top, low = split(jnp.concatenate(pieces, axis=0))
+        second = jnp.dot(
+            jnp.concatenate([top, low, top], axis=1), over_ref[...], preferred_element_type=jnp.float32
+        )
+        spec[pl.ds(pl.multiple_of(line * high, high), high), :] = second[:high]
+        real = second[high:, :LANES]
+        imag = second[high:, LANES:]
+        next_real = after(real)
+        next_imag = after(imag)
+        here = lane == line
+        cos = jnp.sum(jnp.where(here, turned[0], 0.0), axis=1, keepdims=True)[:1]
+        sin = jnp.sum(jnp.where(here, turned[1], 0.0), axis=1, keepdims=True)[:1]
+        numer = numer + (real * next_real + imag * next_imag) * sin
+        numer = numer + (real * next_imag - imag * next_real) * cos
+        denom = denom + (real * real + imag * imag)
+        return numer, denom
+
+    zero = jnp.zeros((high, LANES), jnp.float32)
+    numer, denom = lax.fori_loop(0, lines, forward, (zero, zero), unroll=2)
+    each = value.shape[1]
+    for block in range(count // 2):
+        value[block] = numer[block * each:(block + 1) * each]
+        value[count // 2 + block] = denom[block * each:(block + 1) * each]
+
+    pl.semaphore_wait(barrier, len(peers))
     copies = []
     for step, peer in enumerate(peers):
         copy = pltpu.make_async_remote_copy(
-            src_ref=value_ref.at[ids[step]],
+            src_ref=value.at[ids[step]],
             dst_ref=held.at[step],
             send_sem=send_sem.at[step],
             recv_sem=recv_sem.at[step],
@@ -368,7 +479,7 @@
         )
         copy.start()
         copies.append(copy)
-    total = value_ref[me]
+    total = value[me]
     for step, copy in enumerate(copies):
         copy.wait()
         total = total + held[step]
@@ -387,117 +498,110 @@
         copies.append(copy)
     for copy in copies:
         copy.wait()
-    out_ref[...] = full[...]
-
-
-def total_over(first, second):
+    numer = jnp.concatenate([full[block] for block in range(count // 2)], axis=0)
+    denom = jnp.concatenate([full[count // 2 + block] for block in range(count // 2)], axis=0)
+    slope = numer / (denom + epsilon)
+    below = lax.broadcasted_iota(jnp.int32, (high, high), 1) < lax.broadcasted_iota(jnp.int32, (high, high), 0)
+    ahead = lax.broadcasted_iota(jnp.int32, (LANES, LANES), 0) < lax.broadcasted_iota(jnp.int32, (LANES, LANES), 1)
+    within = exact_dot(below.astype(jnp.float32).astype(jnp.bfloat16), slope)
+    sums = jnp.broadcast_to(jnp.sum(slope, axis=0, keepdims=True), (8, LANES))
+    across = dot_exact(sums, ahead.astype(jnp.float32).astype(jnp.bfloat16))
+    mean = jnp.sum(sums[:1], axis=1, keepdims=True) / length
+    order = lax.broadcasted_iota(jnp.int32, (high, LANES), 0)
+    order = order + high * lax.broadcasted_iota(jnp.int32, (high, LANES), 1)
+    phase = within + across[:1] - order.astype(jnp.float32) * mean
+    phase_ref[...] = phase
+    cos = jnp.cos(phase)
+    sin = jnp.sin(phase)
+
+    def inverse(line, carry):
+        rows = pl.ds(pl.multiple_of(line * high, high), high)
+        real = spec[rows, :LANES]
+        imag = spec[rows, LANES:]
+        fixed = jnp.concatenate([real * cos + imag * sin, imag * cos - real * sin], axis=1)
+        top, low = split(fixed)
+        first = jnp.dot(
+            jnp.concatenate([top, low, top], axis=1), back_ref[...], preferred_element_type=jnp.float32
+        )
+        real = first[:, :LANES]
+        imag = first[:, LANES:]
+        undone = jnp.concatenate(
+            [
+                real * twist_ref[2] - imag * twist_ref[3],
+                real * twist_ref[3] + imag * twist_ref[2],
+            ],
+            axis=0,
+        )
+        top, low = split(undone)
+        grid[pl.ds(pl.multiple_of(line * 2 * high, 2 * high), 2 * high), :] = jnp.dot(
+            up_ref[...], jnp.concatenate([top, low, top], axis=0), preferred_element_type=jnp.float32
+        )
+        return carry
+
+    lax.fori_loop(0, lines, inverse, 0, unroll=2)
+    for half in range(2):
+        for row in range(high):
+            out_ref[half, :, row * LANES:(row + 1) * LANES] = grid[
+                pl.ds(half * high + row, lines, stride=2 * high), :
+            ]
+
+
+def waves(size, modulus, columns):
+    angle = 2.0 * np.pi / modulus * (np.outer(np.arange(size), np.arange(columns)) % modulus)
+    return np.cos(angle), np.sin(angle)
+
+
+def pieces_of(matrix, axis):
+    high = matrix.astype(jnp.bfloat16)
+    low = (matrix - high.astype(np.float64)).astype(jnp.bfloat16)
+    return np.concatenate([high, high, low], axis=axis)
+
+
+def focus(image, centers, halves):
     pings, tiles = lax.axis_size("ping"), lax.axis_size("rng")
     count = pings * tiles
-    length = first.shape[0]
-    value = jnp.concatenate([first, second]).reshape(count, -1, 128)
+    lines, length = image.shape[1:]
+    high = length // LANES
+    cos, sin = waves(high, high, high)
+    down = pieces_of(np.block([[cos, sin], [-sin, cos]]), 1)
+    up = pieces_of(np.block([[cos, -sin], [sin, cos]]), 1)
+    cos, sin = waves(LANES, LANES, LANES)
+    over = pieces_of(np.block([[cos, -sin], [sin, cos]]), 0)
+    back = pieces_of(np.block([[cos, sin], [-sin, cos]]), 0)
+    cos, sin = waves(high, length, LANES)
+    twist = np.stack([cos, sin, cos / length, sin / length]).astype(np.float32)
+    each = 2 * high // count
     vmem = pl.BlockSpec(memory_space=pltpu.VMEM)
+    smem = pl.BlockSpec(memory_space=pltpu.SMEM)
     semaphores = pltpu.SemaphoreType.DMA((count - 1,))
-    total = pl.pallas_call(
-        functools.partial(total_kernel, pings, tiles),
-        out_shape=jax.ShapeDtypeStruct(value.shape, jnp.float32),
-        in_specs=[vmem],
-        out_specs=vmem,
+    focused, phase = pl.pallas_call(
+        functools.partial(focus_kernel, count, tiles),
+        out_shape=(
+            jax.ShapeDtypeStruct((2, lines, length), jnp.float32),
+            jax.ShapeDtypeStruct((high, LANES), jnp.float32),
+        ),
+        in_specs=[smem, smem] + [vmem] * 6,
+        out_specs=(vmem, vmem),
         scratch_shapes=[
-            pltpu.VMEM((count - 1,) + value.shape[1:], jnp.float32),
-            pltpu.VMEM(value.shape, jnp.float32),
+            pltpu.VMEM((lines * 2 * high, LANES), jnp.float32),
+            pltpu.VMEM((lines * high, 2 * LANES), jnp.float32),
+            pltpu.VMEM((count, each, LANES), jnp.float32),
+            pltpu.VMEM((count - 1, each, LANES), jnp.float32),
+            pltpu.VMEM((count, each, LANES), jnp.float32),
+            pltpu.VMEM((2, 8, LANES), jnp.float32),
             semaphores,
             semaphores,
             semaphores,
             semaphores,
         ],
         compiler_params=pltpu.CompilerParams(collective_id=1, has_side_effects=True),
-    )(value).reshape(2, length)
-    return total[0], total[1]
-
-
-def split_length(length):
-    factor_low = 1
-    candidate = 1
-    while candidate * candidate <= length:
-        if length % candidate == 0:
-            factor_low = candidate
-        candidate = candidate + 1
-    return factor_low
-
-
-def table(rows_count, cols_count, modulus, direction):
-    row_ids = jnp.arange(rows_count, dtype=jnp.int32)
-    col_ids = jnp.arange(cols_count, dtype=jnp.int32)
-    product = row_ids[:, None] * col_ids[None, :] % modulus
-    angle = direction * 2.0 * math.pi / modulus * product.astype(jnp.float32)
-    return (jnp.cos(angle), jnp.sin(angle))
-
-
-def transform(real_part, imag_part, direction):
-    length = real_part.shape[-1]
-    size_low = split_length(length)
-    size_high = length // size_low
-    lead_shape = real_part.shape[:-1]
-    highest = lax.Precision.HIGHEST
-    real_grid = real_part.reshape(lead_shape + (size_low, size_high))
-    imag_grid = imag_part.reshape(lead_shape + (size_low, size_high))
-    first_cos, first_sin = table(size_low, size_low, size_low, direction)
-    section_real = jnp.einsum(
-        "kn,...nm->...km", first_cos, real_grid, precision=highest
-    ) - jnp.einsum("kn,...nm->...km", first_sin, imag_grid, precision=highest)
-    section_imag = jnp.einsum(
-        "kn,...nm->...km", first_cos, imag_grid, precision=highest
-    ) + jnp.einsum("kn,...nm->...km", first_sin, real_grid, precision=highest)
-    twist_cos, twist_sin = table(size_low, size_high, length, direction)
-    twisted_real = section_real * twist_cos - section_imag * twist_sin
-    twisted_imag = section_real * twist_sin + section_imag * twist_cos
-    second_cos, second_sin = table(size_high, size_high, size_high, direction)
-    final_real = jnp.einsum(
-        "bm,...km->...bk", second_cos, twisted_real, precision=highest
-    ) - jnp.einsum("bm,...km->...bk", second_sin, twisted_imag, precision=highest)
-    final_imag = jnp.einsum(
-        "bm,...km->...bk", second_cos, twisted_imag, precision=highest
-    ) + jnp.einsum("bm,...km->...bk", second_sin, twisted_real, precision=highest)
-    return (final_real.reshape(lead_shape + (length,)), final_imag.reshape(lead_shape + (length,)))
+    )(centers, halves, down, up, over, back, twist, image)
+    return focused, phase.T.reshape(length)
 
 
 def on_device(echo, steer, offsets, taps, centers, halves):
     image = lines_image(echo, steer, offsets, taps)
-    length = image.shape[2]
-    cells = jnp.arange(length, dtype=jnp.int32)
-    distance = (cells[None, :] - centers[:, None]) % length
-    distance = jnp.minimum(distance, (length - distance) % length)
-    inside = (distance <= halves[:, None]).astype(jnp.float32)
-    stacked_real = jnp.stack([image[0], image[0] * inside])
-    stacked_imag = jnp.stack([image[1], image[1] * inside])
-    spec_real, spec_imag = transform(stacked_real, stacked_imag, -1.0)
-    window_real = spec_real[1]
-    window_imag = spec_imag[1]
-    next_real = jnp.roll(window_real, -1, axis=1)
-    next_imag = jnp.roll(window_imag, -1, axis=1)
-    cross_real = window_real * next_real + window_imag * next_imag
-    cross_imag = window_real * next_imag - window_imag * next_real
-    angle = 2.0 * math.pi / length * centers.astype(jnp.float32)
-    numer_local = jnp.sum(
-        cross_real * jnp.sin(angle)[:, None] + cross_imag * jnp.cos(angle)[:, None], axis=0
-    )
-    denom_local = jnp.sum(window_real * window_real + window_imag * window_imag, axis=0)
-    numer, denom = total_over(numer_local, denom_local)
-    slope = numer / (denom + epsilon)
-    phase_error = (
-        jnp.cumsum(slope)
-        - slope
-        - jnp.arange(length, dtype=jnp.float32) * (jnp.sum(slope) / length)
-    )
-    cos_phase = jnp.cos(phase_error)[None, :]
-    sin_phase = jnp.sin(phase_error)[None, :]
-    full_real = spec_real[0]
-    full_imag = spec_imag[0]
-    fixed_real = full_real * cos_phase + full_imag * sin_phase
-    fixed_imag = full_imag * cos_phase - full_real * sin_phase
-    out_real, out_imag = transform(fixed_real, fixed_imag, 1.0)
-    focused = jnp.stack([out_real, out_imag]) / length
-    return (focused, phase_error)
+    return focus(image, centers, halves)
 
 
 def solution(mesh):

time: 129 us -> 101 us (0.78)
  matrix products: 16.2 us -> 0 us
  local copies, waits for them, and re-layouts: 19.8 us -> 5.16 us
  Pallas kernels: 81.6 us -> 94.4 us
  other arithmetic: 9.1 us -> 0 us
    dot_general x16 -> x0, matrix products: 16.2 us -> none  [the longest x2 2.26 us: transform(): jnp.einsum('bm,...km->...bk', second_sin, twisted_imag, precision=highest)]
    pallas_call x1, Pallas kernels: 17.9 us -> 30.7 us  [focus(): pl.pallas_call(functools.partial(focus_kernel, count, tiles), out_shape=(...]
    slice x10 -> x0, local copies, waits for them, and re-layouts: 6.37 us -> none  [the longest x2 3.18 us: on_device(): window_imag = spec_imag[1]]
    concatenate x6 -> x0, local copies, waits for them, and re-layouts: 5.64 us -> none  [the longest x2 4.77 us: on_device(): next_imag = jnp.roll(window_imag, -1, axis=1)]
    squeeze x4 -> x0, local copies, waits for them, and re-layouts: 3.14 us -> none  [the longest x1 2.37 us: on_device(): window_imag = spec_imag[1]]
    reduce_sum x2 -> x0, other arithmetic: 3.08 us -> none  [the longest x1 1.69 us: on_device(): jnp.sum(cross_real * jnp.sin(angle)[:, None] + cross_imag * jnp.cos(angle...]
    unnamed x1 -> x0, other arithmetic: 1.77 us -> none
    concatenate x3 -> x0, other arithmetic: 1.59 us -> none  [the longest x1 0.87 us: on_device(): next_imag = jnp.roll(window_imag, -1, axis=1)]
where the time goes in v2:
time: 101 us; the launch traced here: 100 us
  Pallas kernels  94.4 us (93%)
  local copies, waits for them, and re-layouts  5.16 us (5%)
    pallas_call x1, Pallas kernels, lines_image(): pl.pallas_call(functools.partial(image_kernel, (tiles, chips, chunks, wid...  63.7 us
    pallas_call x1, Pallas kernels, focus(): pl.pallas_call(functools.partial(focus_kernel, count, tiles), out_shape=(...  30.7 us
    unnamed x2, local copies, waits for them, and re-layouts  3.62 us

profile of v2, /device:TPU:0, one launch (start us, length us, event | category | flops | bytes accessed | tf_op | source)
XLA Modules:
  0.0 100.2 jit_solution(12430933720509996465)
XLA Ops:
  0.6 1.4 %copy.14.taps_ref = f32[16,4]{1,0:T(8,128)} copy(f32[16,4]{0,1:T(4,128)} %param.14) | data formatting | bytes 512 | tf_op args[3]
  2.0 63.7 %shard_map.122.image_ref = f32[2,16,8192]{2,1,0:T(8,128)} custom-call(s32[16]{0:T(128)} %offsets_ref.1, f32[16,4]{1,0:T(8,128)} %copy.14.taps_ref, bf16[2,1024,128]{2,1,0:T(8,128)(2,1)} %echo_ref.1, bf16[2,4096,1024]{2,1,0:T(8,128)(2,1)} %steer_ref.1), custom_call_target="tpu_custom_call" | custom-call | tf_op jit(solution)/shard_map/pallas_call | solution.py:322
  65.7 30.7 %shard_map.123 = (f32[2,16,8192]{2,1,0:T(8,128)}, f32[64,128]{1,0:T(8,128)}) custom-call(s32[16]{0:T(128)} %centers_ref.1, s32[16]{0:T(128)} %halves_ref.1, bf16[128,384]{1,0:T(8,128)(2,1)} %constant.10.clone.down_ref, bf16[128,384]{1,0:T(8,128)(2,1)} %constant.11.clone.up_ref, bf16[768,256]{1,0:T(8,128)(2,1)} %constant.12.clone.over_ref, ...), custom_call_target="tpu_custom_call" | custom-call | tf_op jit(solution)/shard_map/pallas_call | solution.py:577
  96.4 0.8 copy.15
  97.3 0.7 reshape.7
  98.0 2.3 %copy.17 = f32[2,16,8192]{2,1,0:T(8,128)} copy(f32[2,16,8192]{2,1,0:T(8,128)} %get-tuple-element.8) | data formatting | bytes 2097152

commit v3 on v2

v3 whole, which is shorter than its diff:
```python
import functools
import math

import jax
import jax.numpy as jnp
import numpy as np
from jax import lax
from jax.experimental import pallas as pl
from jax.experimental.pallas import tpu as pltpu
from jax.sharding import PartitionSpec as P

PBLK = 64
NTAP = 4


epsilon = 1e-06


MESH = pl.DeviceIdType.MESH


CORES = 2
LAG = 3
EDGE = 32


def encode(value, target):
    count, width = value.shape
    groups = count // 16
    peak = jnp.max(jnp.abs(value), axis=1, keepdims=True)
    power = jnp.floor(jnp.log2(jnp.maximum(peak, 1e-30)) + 1.01)
    whole = jnp.round(value * jnp.exp2(15.0 - power)).astype(jnp.int32).astype(jnp.int16)
    for piece in range(width // 128):
        target[piece * count:(piece + 1) * count, :] = whole[:, piece * 128:(piece + 1) * 128]
    lane = lax.broadcasted_iota(jnp.int32, (16, 128), 1) // (128 // groups)
    powers = jnp.zeros((16, 128), jnp.float32)
    for group in range(groups):
        powers = jnp.where(lane == group, power[group * 16:(group + 1) * 16], powers)
    target[width // 128 * count:, :] = powers.astype(jnp.int32).astype(jnp.int16)


def decode(source, count, width):
    groups = count // 16
    powers = source[width // 128 * count:, :].astype(jnp.int32).astype(jnp.float32)
    scales = jnp.exp2(powers - 15.0)
    span = 128 // groups
    scale = jnp.concatenate(
        [scales[:, group * span:group * span + 1] for group in range(groups)], axis=0
    )
    pieces = [
        source[piece * count:(piece + 1) * count, :].astype(jnp.int32).astype(jnp.float32) * scale
        for piece in range(width // 128)
    ]
    return jnp.concatenate(pieces, axis=1)


def order_of(targets, own):
    return [one for one in targets if one in own] + [one for one in targets if one not in own]


def pick(table, row, column):
    found = jnp.int32(table[0][0])
    for at_row, entries in enumerate(table):
        for at_column, entry in enumerate(entries):
            here = jnp.logical_and(row == at_row, column == at_column)
            found = jnp.where(here, jnp.int32(entry), found)
    return found


def image_kernel(
    plan, offsets_ref, taps_hbm, echo_ref, steer_ref, out_ref,
    taps_ref, held, edge_out, edge_in, left, weights, part, got, away, near, fin, side,
    taps_sem, own_sem, edge_send, edge_recv, echo_send, echo_recv, load_sem, pair_send, pair_recv,
    line_send, line_recv, side_send, side_recv,
):
    tiles, chips, chunks, width, lines, groups = plan
    pings = echo_ref.shape[1]
    columns = echo_ref.shape[2]
    count = tiles * 2 * lines
    share = chips // groups
    me = lax.axis_index("rng")
    chip = lax.axis_index("ping") // CORES
    core = lax.axis_index("ping") % CORES
    last = chips - 1
    partner = {"ping": chip * CORES + 1 - core}
    above = {"ping": (chip + 1) * CORES + core}
    below = {"ping": (chip - 1) * CORES + core}
    peers = [{"rng": lax.rem(me + step, tiles)} for step in range(1, tiles)]

    barrier = pltpu.get_barrier_semaphore()
    for peer in peers + [partner]:
        pl.semaphore_signal(barrier, inc=1, device_id=peer, device_id_type=MESH)

    @pl.when(chip < last)
    def _():
        pl.semaphore_signal(barrier, inc=1, device_id=above, device_id_type=MESH)

    @pl.when(chip > 0)
    def _():
        pl.semaphore_signal(barrier, inc=1, device_id=below, device_id_type=MESH)

    tap_copy = pltpu.make_async_copy(taps_hbm, taps_ref, taps_sem)
    tap_copy.start()
    own = pltpu.make_async_copy(echo_ref, held.at[me], own_sem)
    own.start()

    def load(chunk, half):
        return pltpu.make_async_copy(
            steer_ref.at[half, pl.ds(chunk * width, width), :],
            weights.at[chunk, :, pl.ds(half * pings, pings)],
            load_sem.at[chunk, half],
        )

    for chunk in range(chunks):
        for half in range(2):
            load(chunk, half).start()

    def edge():
        return pltpu.make_async_remote_copy(
            src_ref=edge_out,
            dst_ref=edge_in,
            send_sem=edge_send,
            recv_sem=edge_recv,
            device_id={"rng": lax.rem(me + 1, tiles)},
            device_id_type=MESH,
        )

    if groups > 1:
        def pack(index, carry):
            cols = pl.ds(pl.multiple_of(index * 128, 128), 128)
            for half in range(2):
                value = echo_ref[half, cols, :].astype(jnp.float32).T
                edge_out[half, :, cols] = value[columns - EDGE:].astype(jnp.bfloat16)
            return carry

        lax.fori_loop(0, pings // 128, pack, 0)

    reached = len(peers) + 1 + (chip < last).astype(jnp.int32) + (chip > 0).astype(jnp.int32)
    pl.semaphore_wait(barrier, reached)
    if groups > 1:
        @pl.when(me < tiles - 1)
        def _():
            edge().start()

    copies = []
    for step, peer in enumerate(peers):
        copy = pltpu.make_async_remote_copy(
            src_ref=echo_ref,
            dst_ref=held.at[me],
            send_sem=echo_send.at[step],
            recv_sem=echo_recv.at[step],
            device_id=peer,
            device_id_type=MESH,
        )
        copy.start()
        copies.append(copy)
    own.wait()
    tap_copy.wait()
    column = lax.broadcasted_iota(jnp.int32, (PBLK, 2 * columns), 1)

    def interpolate(tile, before):
        def one(index, carry):
            cols = pl.multiple_of(index * 128, 128)
            turned = []
            for half in range(2):
                ahead = before(half, cols)
                value = held[tile, half, pl.ds(cols, 128), :].astype(jnp.float32)
                value = jnp.concatenate([ahead, value], axis=1)
                blocks = []
                for inner in range(128 // PBLK):
                    block = index * (128 // PBLK) + inner
                    piece = value[inner * PBLK:(inner + 1) * PBLK]
                    offset = offsets_ref[block]
                    result = jnp.zeros((PBLK, columns), jnp.float32)
                    for tap in range(NTAP):
                        moved = pltpu.roll(piece, offset + tap, axis=1)[:, columns:]
                        result = result + taps_ref[tap, block] * moved
                    blocks.append(result)
                turned.append(jnp.concatenate(blocks, axis=0).T)
            real, imag = turned
            for piece in range(columns // lines):
                row = tile * (columns // lines) + piece
                owner = row // tiles
                target = owner // CORES
                place = (target // share * CORES + owner % CORES) * share + target % share
                place = pl.multiple_of((place * tiles + row % tiles) * 2 * lines, 2 * lines)
                a = real[piece * lines:(piece + 1) * lines].astype(jnp.bfloat16)
                b = imag[piece * lines:(piece + 1) * lines].astype(jnp.bfloat16)
                left[pl.ds(place, lines), pl.ds(cols, 128)] = a
                left[pl.ds(place + lines, lines), pl.ds(cols, 128)] = b
                left[pl.ds(place, lines), pl.ds(pings + cols, 128)] = -b
                left[pl.ds(place + lines, lines), pl.ds(pings + cols, 128)] = a
            return carry

        lax.fori_loop(0, pings // 128, one, 0)

    def from_edge(half, cols):
        value = edge_in[half, :, pl.ds(cols, 128)].astype(jnp.float32)
        value = jnp.where(me > 0, value, 0.0)
        return jnp.concatenate([jnp.zeros((columns - EDGE, 128), jnp.float32), value], axis=0).T

    def from_tile(tile):
        def before(half, cols):
            value = held[lax.max(tile - 1, 0), half, pl.ds(cols, 128), :].astype(jnp.float32)
            return jnp.where(tile > 0, value, 0.0)

        return before

    def pair(group, chunk):
        rows = pl.ds(pl.multiple_of(group * share * count, share * count), share * count)
        return pltpu.make_async_remote_copy(
            src_ref=part.at[chunk, 1 - core, rows],
            dst_ref=got.at[chunk, rows],
            send_sem=pair_send.at[group, chunk],
            recv_sem=pair_recv.at[group, chunk],
            device_id=partner,
            device_id_type=MESH,
        )

    def line(way, target, chunk):
        return pltpu.make_async_remote_copy(
            src_ref=away.at[way, target, chunk],
            dst_ref=near.at[way, target, chunk],
            send_sem=line_send.at[way, target, chunk],
            recv_sem=line_recv.at[way, target, chunk],
            device_id=(above, below)[way],
            device_id_type=MESH,
        )

    def rows_of(target):
        return pl.ds(pl.multiple_of(target * count, count), count)

    def collect(way, target, chunk):
        line(way, target, chunk).wait_recv()
        part[chunk, core, rows_of(target), :] += decode(near.at[way, target, chunk], count, width)

    def pass_on(way, target, chunk, first):
        @pl.when(jnp.logical_not(first))
        def _():
            collect(way, target, chunk)

        encode(part[chunk, core, rows_of(target), :], away.at[way, target, chunk])
        line(way, target, chunk).start()

    half_rows = share * count
    block = min(512, CORES * half_rows)

    def multiply(group, chunk, first):
        if first:
            for half in range(2):
                load(chunk, half).wait()
        base = group * CORES * half_rows
        if block == CORES * half_rows:
            rows = pl.ds(pl.multiple_of(base, block), block)
            value = lax.dot_general(
                left[rows, :], weights[chunk], (((1,), (1,)), ((), ())),
                preferred_element_type=jnp.float32,
            )
            into = pl.ds(pl.multiple_of(group * half_rows, half_rows), half_rows)
            part[chunk, 0, into, :] = value[:half_rows]
            part[chunk, 1, into, :] = value[half_rows:]
        else:
            def rows_at(index, carry):
                rows = pl.ds(pl.multiple_of(base + index * block, block), block)
                value = lax.dot_general(
                    left[rows, :], weights[chunk], (((1,), (1,)), ((), ())),
                    preferred_element_type=jnp.float32,
                )
                start = group * half_rows + index % (half_rows // block) * block
                into = pl.ds(pl.multiple_of(start, block), block)
                part[chunk, index // (half_rows // block), into, :] = value
                return carry

            lax.fori_loop(0, CORES * half_rows // block, rows_at, 0)
        pair(group, chunk).start()

    def join(group, chunk):
        pair(group, chunk).wait_recv()
        rows = pl.ds(pl.multiple_of(group * half_rows, half_rows), half_rows)
        part[chunk, core, rows, :] += got[chunk, rows, :]

    tables = []
    for way in range(2):
        far_first = (list(range(last, 0, -1)), list(range(last)))[way]
        tables.append(
            [
                order_of(far_first, range(group * share, (group + 1) * share))
                for group in range(groups)
            ]
        )

    def across(step, chunk):
        peer = lax.rem(me + step, tiles)
        return pltpu.make_async_remote_copy(
            src_ref=fin.at[chunk, peer],
            dst_ref=side.at[chunk, step - 1],
            send_sem=side_send.at[step - 1, chunk],
            recv_sem=side_recv.at[step - 1, chunk],
            device_id={"rng": peer},
            device_id_type=MESH,
        )

    def place(source, chunk, value):
        start = pl.multiple_of(source * (chunks * width) + chunk * width, width)
        out_ref[0, :, pl.ds(start, width)] = value[:lines]
        out_ref[1, :, pl.ds(start, width)] = value[lines:]

    def finish(chunk):
        @pl.when(chip > 0)
        def _():
            collect(0, chip, chunk)

        @pl.when(chip < last)
        def _():
            collect(1, chip, chunk)

        for tile in range(tiles):
            rows = pl.ds(pl.multiple_of(chip * count + tile * 2 * lines, 2 * lines), 2 * lines)
            fin[chunk, tile] = part[chunk, core, rows, :]
        for step in range(1, tiles):
            across(step, chunk).start()
        place(me, chunk, fin[chunk, me])

    begins = []
    for way in range(2):
        begins.append(
            [
                [
                    row.index(target) * chunks + (target, last - target)[way] * LAG if target in row else 0
                    for target in range(chips)
                ]
                for row in tables[way]
            ]
        )
    mine = me if groups > 1 else 0
    begin = jnp.maximum(pick(begins[0], mine, chip), pick(begins[1], mine, chip))

    def stream(time):
        for way in range(2):
            hops = (chip, last - chip)[way]
            at = time - hops * LAG
            target = pick(tables[way], mine, at // chunks)
            ahead = (chip < target, chip > target)[way]
            ready = jnp.logical_and(at >= 0, at < last * chunks)

            @pl.when(jnp.logical_and(ready, ahead))
            def _():
                pass_on(way, target, at % chunks, hops == 0)

        done = time - begin

        @pl.when(jnp.logical_and(done >= 0, done < chunks))
        def _():
            finish(done)

    def steps(group, turn):
        def one(chunk, carry):
            multiply(group, chunk, turn == 0)

            @pl.when(chunk > 0)
            def _():
                join(group, chunk - 1)
                stream(turn * chunks + chunk - 1)

            return carry

        lax.fori_loop(0, chunks, one, 0)
        join(group, chunks - 1)
        stream(turn * chunks + chunks - 1)

    if groups > 1:
        @pl.when(me > 0)
        def _():
            edge().wait_recv()

        interpolate(me, from_edge)
        steps(me, 0)
        for step, copy in enumerate(copies):
            source = lax.rem(me + tiles - 1 - step, tiles)
            copy.wait_recv()
        for step, copy in enumerate(copies):
            source = lax.rem(me + tiles - 1 - step, tiles)
            interpolate(source, from_tile(source))
            steps(source, 1 + step)
    else:
        for copy in copies:
            copy.wait_recv()

        def each(tile, carry):
            interpolate(tile, from_tile(tile))
            return carry

        lax.fori_loop(0, tiles, each, 0)
        steps(0, 0)

    def rest(time, carry):
        stream(time)
        return carry

    lax.fori_loop(groups * chunks, last * chunks + last * LAG, rest, 0)

    def arrive(chunk, carry):
        for step in range(1, tiles):
            across(step, chunk).wait()
            place(lax.rem(me + tiles - step, tiles), chunk, side[chunk, step - 1])
        for group in range(groups):
            pair(group, chunk).wait_send()
        for way in range(2):
            for target in range(chips):
                ahead = (chip < target, chip > target)[way]

                @pl.when(ahead)
                def _():
                    line(way, target, chunk).wait_send()

        return carry

    lax.fori_loop(0, chunks, arrive, 0)
    for copy in copies:
        copy.wait_send()
    if groups > 1:
        @pl.when(me < tiles - 1)
        def _():
            edge().wait_send()


def lines_image(echo, steer, offsets, taps):
    tiles = lax.axis_size("rng")
    chips = lax.axis_size("ping") // CORES
    pings, columns = echo.shape[1:]
    cells = steer.shape[1]
    width = 512 if cells % 4096 == 0 else 256
    chunks = cells // width
    lines = columns // (chips * CORES)
    count = tiles * 2 * lines
    rows = chips * count
    groups = tiles if chips % tiles == 0 else 1
    vmem = pl.BlockSpec(memory_space=pltpu.VMEM)
    smem = pl.BlockSpec(memory_space=pltpu.SMEM)
    anywhere = pl.BlockSpec(memory_space=pl.ANY)
    dma = pltpu.SemaphoreType.DMA
    message = (width // 128 * count + 16, 128)
    others = max(tiles - 1, 1)
    return pl.pallas_call(
        functools.partial(image_kernel, (tiles, chips, chunks, width, lines, groups)),
        out_shape=jax.ShapeDtypeStruct((2, lines, tiles * cells), jnp.float32),
        in_specs=[smem, anywhere, vmem, anywhere],
        out_specs=vmem,
        scratch_shapes=[
            pltpu.SMEM(taps.shape[::-1], jnp.float32),
            pltpu.VMEM((tiles, 2, pings, columns), jnp.bfloat16),
            pltpu.VMEM((2, EDGE, pings), jnp.bfloat16),
            pltpu.VMEM((2, EDGE, pings), jnp.bfloat16),
            pltpu.VMEM((CORES * rows, 2 * pings), jnp.bfloat16),
            pltpu.VMEM((chunks, width, 2 * pings), jnp.bfloat16),
            pltpu.VMEM((chunks, CORES, rows, width), jnp.float32),
            pltpu.VMEM((chunks, rows, width), jnp.float32),
            pltpu.VMEM((2, chips, chunks) + message, jnp.int16),
            pltpu.VMEM((2, chips, chunks) + message, jnp.int16),
            pltpu.VMEM((chunks, tiles, 2 * lines, width), jnp.float32),
            pltpu.VMEM((chunks, others, 2 * lines, width), jnp.float32),
            dma,
            dma,
            dma,
            dma,
            dma((others,)),
            dma((others,)),
            dma((chunks, 2)),
            dma((groups, chunks)),
            dma((groups, chunks)),
            dma((2, chips, chunks)),
            dma((2, chips, chunks)),
            dma((others, chunks)),
            dma((others, chunks)),
        ],
        compiler_params=pltpu.CompilerParams(
            collective_id=0, has_side_effects=True, vmem_limit_bytes=60 * 2**20
        ),
    )(offsets, taps.T, echo, steer)


LANES = 128
BATCH = 4


def split(value):
    high = value.astype(jnp.bfloat16)
    return high, (value - high.astype(jnp.float32)).astype(jnp.bfloat16)


def exact_dot(left, right):
    total = None
    for _ in range(3):
        piece = right.astype(jnp.bfloat16)
        term = jnp.dot(left, piece, preferred_element_type=jnp.float32)
        total = term if total is None else total + term
        right = right - piece.astype(jnp.float32)
    return total


def dot_exact(left, right):
    total = None
    for _ in range(3):
        piece = left.astype(jnp.bfloat16)
        term = jnp.dot(piece, right, preferred_element_type=jnp.float32)
        total = term if total is None else total + term
        left = left - piece.astype(jnp.float32)
    return total


def stacked(value, axis):
    top, low = split(value)
    return jnp.concatenate([top, low, top], axis=axis)


def spectrum_of(fields, down_ref, over_ref, twist_ref):
    size = len(fields)
    high = fields[0].shape[0] // 2
    first = jnp.dot(
        down_ref[...], stacked(jnp.concatenate(fields, axis=1), 0), preferred_element_type=jnp.float32
    )
    rows = []
    for one in range(size):
        real = first[:high, one * LANES:(one + 1) * LANES]
        imag = first[high:, one * LANES:(one + 1) * LANES]
        rows.append(
            jnp.concatenate(
                [
                    real * twist_ref[0] + imag * twist_ref[1],
                    imag * twist_ref[0] - real * twist_ref[1],
                ],
                axis=1,
            )
        )
    return jnp.dot(
        stacked(jnp.concatenate(rows, axis=0), 1), over_ref[...], preferred_element_type=jnp.float32
    )


def gradient_kernel(
    count, tiles, centers_ref, halves_ref, down_ref, over_ref, twist_ref, image_ref, total_ref, spec_ref,
    grid, value, held, full, turned, send_sem, recv_sem, send_two, recv_two,
):
    me = lax.axis_index("ping") * tiles + lax.axis_index("rng")
    ids = [lax.rem(me + step, count) for step in range(1, count)]
    peers = [{"ping": lax.div(one, tiles), "rng": lax.rem(one, tiles)} for one in ids]
    barrier = pltpu.get_barrier_semaphore()
    for peer in peers:
        pl.semaphore_signal(barrier, inc=1, device_id=peer, device_id_type=MESH)

    lines, length = image_ref.shape[1:]
    high = length // LANES
    for half in range(2):
        for row in range(high):
            grid[pl.ds(half * high + row, lines, stride=2 * high), :] = image_ref[
                half, :, row * LANES:(row + 1) * LANES
            ]

    cells = lax.broadcasted_iota(jnp.int32, (high, LANES), 0) * LANES
    cells = cells + lax.broadcasted_iota(jnp.int32, (high, LANES), 1)
    bottom = lax.broadcasted_iota(jnp.int32, (8, LANES), 0) == 7
    lane = lax.broadcasted_iota(jnp.int32, (8, LANES), 1)
    angle = jnp.zeros((8, LANES), jnp.float32)
    for line in range(lines):
        angle = jnp.where(lane == line, centers_ref[line].astype(jnp.float32), angle)
    angle = angle * (2.0 * math.pi / length)
    turned[0] = jnp.cos(angle)
    turned[1] = jnp.sin(angle)

    def after(part):
        moved = pltpu.roll(part, high - 1, axis=0)
        end = moved[high - 8:]
        end = jnp.where(bottom, pltpu.roll(end, LANES - 1, axis=1), end)
        return jnp.concatenate([moved[:high - 8], end], axis=0)

    def field(line):
        return grid[pl.ds(pl.multiple_of(line * 2 * high, 2 * high), 2 * high), :]

    def windowed(index, carry):
        numer, denom = carry
        chosen = []
        for inner in range(BATCH):
            line = index * BATCH + inner
            distance = cells - centers_ref[line]
            distance = jnp.where(distance < 0, distance + length, distance)
            distance = jnp.minimum(distance, length - distance)
            inside = (distance <= halves_ref[line]).astype(jnp.float32)
            chosen.append(field(line) * jnp.concatenate([inside, inside], axis=0))
        found = spectrum_of(chosen, down_ref, over_ref, twist_ref)
        for inner in range(BATCH):
            real = found[inner * high:(inner + 1) * high, :LANES]
            imag = found[inner * high:(inner + 1) * high, LANES:]
            next_real = after(real)
            next_imag = after(imag)
            here = lane == index * BATCH + inner
            cos = jnp.sum(jnp.where(here, turned[0], 0.0), axis=1, keepdims=True)[:1]
            sin = jnp.sum(jnp.where(here, turned[1], 0.0), axis=1, keepdims=True)[:1]
            numer = numer + (real * next_real + imag * next_imag) * sin
            numer = numer + (real * next_imag - imag * next_real) * cos
            denom = denom + (real * real + imag * imag)
        return numer, denom

    zero = jnp.zeros((high, LANES), jnp.float32)
    numer, denom = lax.fori_loop(0, lines // BATCH, windowed, (zero, zero))
    each = value.shape[1]
    for block in range(count // 2):
        value[block] = numer[block * each:(block + 1) * each]
        value[count // 2 + block] = denom[block * each:(block + 1) * each]

    pl.semaphore_wait(barrier, len(peers))
    copies = []
    for step, peer in enumerate(peers):
        copy = pltpu.make_async_remote_copy(
            src_ref=value.at[ids[step]],
            dst_ref=held.at[step],
            send_sem=send_sem.at[step],
            recv_sem=recv_sem.at[step],
            device_id=peer,
            device_id_type=MESH,
        )
        copy.start()
        copies.append(copy)

    def whole(index, carry):
        found = spectrum_of(
            [field(index * BATCH + inner) for inner in range(BATCH)], down_ref, over_ref, twist_ref
        )
        spec_ref[pl.ds(pl.multiple_of(index * BATCH * high, BATCH * high), BATCH * high), :] = found
        return carry

    lax.fori_loop(0, lines // BATCH, whole, 0)
    total = value[me]
    for step, copy in enumerate(copies):
        copy.wait()
        total = total + held[step]
    full[me] = total
    copies = []
    for step, peer in enumerate(peers):
        copy = pltpu.make_async_remote_copy(
            src_ref=full.at[me],
            dst_ref=full.at[me],
            send_sem=send_two.at[step],
            recv_sem=recv_two.at[step],
            device_id=peer,
            device_id_type=MESH,
        )
        copy.start()
        copies.append(copy)
    for copy in copies:
        copy.wait()
    for block in range(count):
        total_ref[block * each:(block + 1) * each, :] = full[block]


def correct_kernel(
    up_ref, back_ref, twist_ref, total_ref, spec_ref, out_ref, phase_ref, grid, turn, tall,
):
    group = out_ref.shape[1]
    length = out_ref.shape[2]
    high = length // LANES

    @pl.when(pl.program_id(0) == 0)
    def _():
        slope = total_ref[:high] / (total_ref[high:] + epsilon)
        row = lax.broadcasted_iota(jnp.int32, (high, high), 0)
        below = (lax.broadcasted_iota(jnp.int32, (high, high), 1) < row).astype(jnp.float32)
        row = lax.broadcasted_iota(jnp.int32, (LANES, LANES), 0)
        ahead = (row < lax.broadcasted_iota(jnp.int32, (LANES, LANES), 1)).astype(jnp.float32)
        within = exact_dot(below.astype(jnp.bfloat16), slope)
        sums = jnp.broadcast_to(jnp.sum(slope, axis=0, keepdims=True), (8, LANES))
        across = dot_exact(sums, ahead.astype(jnp.bfloat16))
        mean = jnp.sum(sums[:1], axis=1, keepdims=True) / length
        order = lax.broadcasted_iota(jnp.int32, (high, LANES), 0)
        order = order + high * lax.broadcasted_iota(jnp.int32, (high, LANES), 1)
        phase = within + across[:1] - order.astype(jnp.float32) * mean
        ratio = LANES // high
        tall[:, :high] = phase.T
        phase_ref[...] = jnp.concatenate(
            [tall[pl.ds(part, LANES // ratio, stride=ratio), :high] for part in range(ratio)], axis=1
        )
        turn[0] = jnp.cos(phase)
        turn[1] = jnp.sin(phase)

    cos = turn[0]
    sin = turn[1]
    start = pl.program_id(0) * group * high
    rows = []
    for line in range(group):
        at = pl.ds(pl.multiple_of(start + line * high, high), high)
        real = spec_ref[at, :LANES]
        imag = spec_ref[at, LANES:]
        rows.append(jnp.concatenate([real * cos + imag * sin, imag * cos - real * sin], axis=1))
    first = jnp.dot(
        stacked(jnp.concatenate(rows, axis=0), 1), back_ref[...], preferred_element_type=jnp.float32
    )
    fields = []
    for line in range(group):
        real = first[line * high:(line + 1) * high, :LANES]
        imag = first[line * high:(line + 1) * high, LANES:]
        fields.append(
            jnp.concatenate(
                [
                    real * twist_ref[2] - imag * twist_ref[3],
                    real * twist_ref[3] + imag * twist_ref[2],
                ],
                axis=0,
            )
        )
    second = jnp.dot(
        up_ref[...], stacked(jnp.concatenate(fields, axis=1), 0), preferred_element_type=jnp.float32
    )
    for line in range(group):
        grid[line * 2 * high:(line + 1) * 2 * high, :] = second[:, line * LANES:(line + 1) * LANES]
    for half in range(2):
        for row in range(high):
            out_ref[half, :, row * LANES:(row + 1) * LANES] = grid[
                pl.ds(half * high + row, group, stride=2 * high), :
            ]


def waves(size, modulus, columns):
    angle = 2.0 * np.pi / modulus * (np.outer(np.arange(size), np.arange(columns)) % modulus)
    return np.cos(angle), np.sin(angle)


def pieces_of(matrix, axis):
    high = matrix.astype(jnp.bfloat16)
    low = (matrix - high.astype(np.float64)).astype(jnp.bfloat16)
    return np.concatenate([high, high, low], axis=axis)


def focus(image, centers, halves):
    pings, tiles = lax.axis_size("ping"), lax.axis_size("rng")
    count = pings * tiles
    lines, length = image.shape[1:]
    high = length // LANES
    cos, sin = waves(high, high, high)
    down = pieces_of(np.block([[cos, sin], [-sin, cos]]), 1)
    up = pieces_of(np.block([[cos, -sin], [sin, cos]]), 1)
    cos, sin = waves(LANES, LANES, LANES)
    over = pieces_of(np.block([[cos, -sin], [sin, cos]]), 0)
    back = pieces_of(np.block([[cos, sin], [-sin, cos]]), 0)
    cos, sin = waves(high, length, LANES)
    twist = np.stack([cos, sin, cos / length, sin / length]).astype(np.float32)
    each = 2 * high // count
    group = 8
    vmem = pl.BlockSpec(memory_space=pltpu.VMEM)
    smem = pl.BlockSpec(memory_space=pltpu.SMEM)
    semaphores = pltpu.SemaphoreType.DMA((count - 1,))
    total, spec = pl.pallas_call(
        functools.partial(gradient_kernel, count, tiles),
        out_shape=(
            jax.ShapeDtypeStruct((2 * high, LANES), jnp.float32),
            jax.ShapeDtypeStruct((lines * high, 2 * LANES), jnp.float32),
        ),
        in_specs=[smem, smem] + [vmem] * 4,
        out_specs=(vmem, vmem),
        scratch_shapes=[
            pltpu.VMEM((lines * 2 * high, LANES), jnp.float32),
            pltpu.VMEM((count, each, LANES), jnp.float32),
            pltpu.VMEM((count - 1, each, LANES), jnp.float32),
            pltpu.VMEM((count, each, LANES), jnp.float32),
            pltpu.VMEM((2, 8, LANES), jnp.float32),
            semaphores,
            semaphores,
            semaphores,
            semaphores,
        ],
        compiler_params=pltpu.CompilerParams(collective_id=1, has_side_effects=True),
    )(centers, halves, down, over, twist, image)
    focused, phase = pl.pallas_call(
        correct_kernel,
        grid=(lines // group,),
        out_shape=(
            jax.ShapeDtypeStruct((2, lines, length), jnp.float32),
            jax.ShapeDtypeStruct((high, LANES), jnp.float32),
        ),
        in_specs=[vmem] * 5,
        out_specs=(
            pl.BlockSpec((2, group, length), lambda index: (0, index, 0)),
            pl.BlockSpec((high, LANES), lambda index: (0, 0)),
        ),
        scratch_shapes=[
            pltpu.VMEM((group * 2 * high, LANES), jnp.float32),
            pltpu.VMEM((2, high, LANES), jnp.float32),
            pltpu.VMEM((LANES, LANES), jnp.float32),
        ],
    )(up, back, twist, total, spec)
    return focused, phase.reshape(length)


def on_device(echo, steer, offsets, taps, centers, halves):
    image = lines_image(echo, steer, offsets, taps)
    return focus(image, centers, halves)


def solution(mesh):
    in_specs = (
        P(None, ("leg", "ping"), "rng"),
        P(None, ("leg", "rng"), "ping"),
        P(("leg", "ping")),
        P(("leg", "ping"), None),
        P(("leg", "ping", "rng")),
        P(("leg", "ping", "rng")),
    )
    out_specs = (P(None, ("leg", "ping", "rng"), None), P("leg"))
    return jax.shard_map(
        on_device, mesh=mesh, in_specs=in_specs, out_specs=out_specs, check_vma=False
    )
```

time: 101 us -> 87.4 us (0.87)
  Pallas kernels: 94.4 us -> 86.6 us
  local copies, waits for them, and re-layouts: 5.16 us -> 0 us
    pallas_call x1, Pallas kernels: 63.7 us -> 59.1 us  [lines_image(): pl.pallas_call(functools.partial(image_kernel, (tiles, chips, chunks, wid...]
    unnamed x2 -> x0, local copies, waits for them, and re-layouts: 3.62 us -> none
    pallas_call x1 -> x2, Pallas kernels: 30.7 us -> 27.5 us  [the longest x1 22.6 us: focus(): pl.pallas_call(functools.partial(gradient_kernel, count, tiles), out_shap...]
where the time goes in v3:
time: 87.4 us; the launch traced here: 87.2 us
  Pallas kernels  86.6 us (99%)
    pallas_call x1, Pallas kernels, lines_image(): pl.pallas_call(functools.partial(image_kernel, (tiles, chips, chunks, wid...  59.1 us
    pallas_call x1, Pallas kernels, focus(): pl.pallas_call(functools.partial(gradient_kernel, count, tiles), out_shap...  22.6 us
    pallas_call x1, Pallas kernels, focus(): pl.pallas_call(correct_kernel, grid=(lines // group,), out_shape=(jax.Sha...  4.86 us

profile of v3, /device:TPU:0, one launch (start us, length us, event | category | flops | bytes accessed | tf_op | source)
XLA Modules:
  0.0 87.2 jit_solution(10814522279307168401)
XLA Ops:
  0.6 59.1 %shard_map.122.image_ref = f32[2,16,8192]{2,1,0:T(8,128)} custom-call(s32[16]{0:T(128)} %offsets_ref.1, f32[4,16]{1,0:T(4,128)} %bitcast.2, bf16[2,1024,128]{2,1,0:T(8,128)(2,1)} %echo_ref.1, bf16[2,4096,1024]{2,1,0:T(8,128)(2,1)} %steer_ref.1), custom_call_target="tpu_custom_call" | custom-call | tf_op jit(solution)/shard_map/pallas_call | solution.py:444
  59.7 22.6 %shard_map.123 = (f32[128,128]{1,0:T(8,128)}, f32[1024,256]{1,0:T(8,128)}) custom-call(s32[16]{0:T(128)} %centers_ref.1, s32[16]{0:T(128)} %halves_ref.1, bf16[128,384]{1,0:T(8,128)(2,1)} %constant.10.clone.down_ref, bf16[768,256]{1,0:T(8,128)(2,1)} %constant.11.clone.over_ref, f32[4,64,128]{2,1,0:T(8,128)} %constant.12.clone.twist_ref, ...), custom_call_target="tpu_custom_call" | custom-call | tf_op jit(solution)/shard_map/pallas_call | solution.py:750
  82.4 4.9 %shard_map.124 = (f32[2,16,8192]{2,1,0:T(8,128)}, f32[64,128]{1,0:T(8,128)}) custom-call(bf16[128,384]{1,0:T(8,128)(2,1)} %constant.13.clone.up_ref, bf16[768,256]{1,0:T(8,128)(2,1)} %constant.14.clone.back_ref, f32[4,64,128]{2,1,0:T(8,128)} %constant.12.clone.twist_ref, f32[128,128]{1,0:T(8,128)} %get-tuple-element.6.total_ref, ...), custom_call_target="tpu_custom_call" | custom-call | tf_op jit(solution)/shard_map/pallas_call | solution.py:771

commit v4 on v3

--- a/solution.py
+++ b/solution.py
@@ -24,29 +24,30 @@
 EDGE = 32
 
 
-def encode(value, target):
+def encode(value, target, scales):
     count, width = value.shape
-    groups = count // 16
     peak = jnp.max(jnp.abs(value), axis=1, keepdims=True)
     power = jnp.floor(jnp.log2(jnp.maximum(peak, 1e-30)) + 1.01)
     whole = jnp.round(value * jnp.exp2(15.0 - power)).astype(jnp.int32).astype(jnp.int16)
     for piece in range(width // 128):
         target[piece * count:(piece + 1) * count, :] = whole[:, piece * 128:(piece + 1) * 128]
-    lane = lax.broadcasted_iota(jnp.int32, (16, 128), 1) // (128 // groups)
-    powers = jnp.zeros((16, 128), jnp.float32)
-    for group in range(groups):
-        powers = jnp.where(lane == group, power[group * 16:(group + 1) * 16], powers)
-    target[width // 128 * count:, :] = powers.astype(jnp.int32).astype(jnp.int16)
-
-
-def decode(source, count, width):
-    groups = count // 16
-    powers = source[width // 128 * count:, :].astype(jnp.int32).astype(jnp.float32)
-    scales = jnp.exp2(powers - 15.0)
-    span = 128 // groups
-    scale = jnp.concatenate(
-        [scales[:, group * span:group * span + 1] for group in range(groups)], axis=0
-    )
+    size = min(count, 128)
+    lane = lax.broadcasted_iota(jnp.int32, (size, 128), 1)
+    here = lane == lax.broadcasted_iota(jnp.int32, (size, 128), 0)
+    for piece in range(count // size):
+        part = jnp.where(here, power[piece * size:(piece + 1) * size], 0.0)
+        scales[piece:piece + 1, :] = jnp.sum(part, axis=0, keepdims=True)
+
+
+def decode(source, scales, count, width):
+    size = min(count, 128)
+    lane = lax.broadcasted_iota(jnp.int32, (size, 128), 1)
+    here = lane == lax.broadcasted_iota(jnp.int32, (size, 128), 0)
+    powers = [
+        jnp.sum(jnp.where(here, scales[piece:piece + 1, :], 0.0), axis=1, keepdims=True)
+        for piece in range(count // size)
+    ]
+    scale = jnp.exp2(jnp.concatenate(powers, axis=0) - 15.0)
     pieces = [
         source[piece * count:(piece + 1) * count, :].astype(jnp.int32).astype(jnp.float32) * scale
         for piece in range(width // 128)
@@ -69,9 +70,9 @@
 
 def image_kernel(
     plan, offsets_ref, taps_hbm, echo_ref, steer_ref, out_ref,
-    taps_ref, held, edge_out, edge_in, left, weights, part, got, away, near, fin, side,
+    taps_ref, held, edge_out, edge_in, left, weights, part, got, away, near, away_scale, near_scale, fin, side,
     taps_sem, own_sem, edge_send, edge_recv, echo_send, echo_recv, load_sem, pair_send, pair_recv,
-    line_send, line_recv, side_send, side_recv,
+    line_send, line_recv, scale_send, scale_recv, side_send, side_recv,
 ):
     tiles, chips, chunks, width, lines, groups = plan
     pings = echo_ref.shape[1]
@@ -125,12 +126,20 @@
             device_id_type=MESH,
         )
 
+    row = lax.broadcasted_iota(jnp.int32, (128, 128), 0)
+    unit = (row == lax.broadcasted_iota(jnp.int32, (128, 128), 1)).astype(jnp.float32).astype(jnp.bfloat16)
+
+    def turn(chosen, value):
+        return lax.dot_general(
+            chosen, value, (((1,), (1,)), ((), ())), preferred_element_type=jnp.float32
+        )
+
     if groups > 1:
         def pack(index, carry):
             cols = pl.ds(pl.multiple_of(index * 128, 128), 128)
             for half in range(2):
-                value = echo_ref[half, cols, :].astype(jnp.float32).T
-                edge_out[half, :, cols] = value[columns - EDGE:].astype(jnp.bfloat16)
+                value = turn(unit[columns - EDGE:], echo_ref[half, cols, :])
+                edge_out[half, :, cols] = value.astype(jnp.bfloat16)
             return carry
 
         lax.fori_loop(0, pings // 128, pack, 0)
@@ -176,7 +185,7 @@
                         moved = pltpu.roll(piece, offset + tap, axis=1)[:, columns:]
                         result = result + taps_ref[tap, block] * moved
                     blocks.append(result)
-                turned.append(jnp.concatenate(blocks, axis=0).T)
+                turned.append(turn(unit, jnp.concatenate(blocks, axis=0).astype(jnp.bfloat16)).astype(jnp.bfloat16))
             real, imag = turned
             for piece in range(columns // lines):
                 row = tile * (columns // lines) + piece
@@ -184,20 +193,21 @@
                 target = owner // CORES
                 place = (target // share * CORES + owner % CORES) * share + target % share
                 place = pl.multiple_of((place * tiles + row % tiles) * 2 * lines, 2 * lines)
-                a = real[piece * lines:(piece + 1) * lines].astype(jnp.bfloat16)
-                b = imag[piece * lines:(piece + 1) * lines].astype(jnp.bfloat16)
+                a = real[piece * lines:(piece + 1) * lines]
+                b = imag[piece * lines:(piece + 1) * lines]
                 left[pl.ds(place, lines), pl.ds(cols, 128)] = a
                 left[pl.ds(place + lines, lines), pl.ds(cols, 128)] = b
                 left[pl.ds(place, lines), pl.ds(pings + cols, 128)] = -b
                 left[pl.ds(place + lines, lines), pl.ds(pings + cols, 128)] = a
             return carry
 
-        lax.fori_loop(0, pings // 128, one, 0)
+        lax.fori_loop(0, pings // 128, one, 0, unroll=2)
 
     def from_edge(half, cols):
         value = edge_in[half, :, pl.ds(cols, 128)].astype(jnp.float32)
-        value = jnp.where(me > 0, value, 0.0)
-        return jnp.concatenate([jnp.zeros((columns - EDGE, 128), jnp.float32), value], axis=0).T
+        value = jnp.where(me > 0, value, 0.0).astype(jnp.bfloat16)
+        value = jnp.concatenate([jnp.zeros((columns - EDGE, 128), jnp.bfloat16), value], axis=0)
+        return turn(unit, value)
 
     def from_tile(tile):
         def before(half, cols):
@@ -227,19 +237,35 @@
             device_id_type=MESH,
         )
 
+    def scale_line(way, target, chunk):
+        return pltpu.make_async_remote_copy(
+            src_ref=away_scale.at[way, target, chunk],
+            dst_ref=near_scale.at[way, target, chunk],
+            send_sem=scale_send.at[way, target, chunk],
+            recv_sem=scale_recv.at[way, target, chunk],
+            device_id=(above, below)[way],
+            device_id_type=MESH,
+        )
+
     def rows_of(target):
         return pl.ds(pl.multiple_of(target * count, count), count)
 
     def collect(way, target, chunk):
+        scale_line(way, target, chunk).wait_recv()
         line(way, target, chunk).wait_recv()
-        part[chunk, core, rows_of(target), :] += decode(near.at[way, target, chunk], count, width)
+        part[chunk, core, rows_of(target), :] += decode(
+            near.at[way, target, chunk], near_scale.at[way, target, chunk], count, width
+        )
 
     def pass_on(way, target, chunk, first):
         @pl.when(jnp.logical_not(first))
         def _():
             collect(way, target, chunk)
 
-        encode(part[chunk, core, rows_of(target), :], away.at[way, target, chunk])
+        encode(
+            part[chunk, core, rows_of(target), :], away.at[way, target, chunk], away_scale.at[way, target, chunk]
+        )
+        scale_line(way, target, chunk).start()
         line(way, target, chunk).start()
 
     half_rows = share * count
@@ -412,6 +438,7 @@
                 @pl.when(ahead)
                 def _():
                     line(way, target, chunk).wait_send()
+                    scale_line(way, target, chunk).wait_send()
 
         return carry
 
@@ -439,7 +466,8 @@
     smem = pl.BlockSpec(memory_space=pltpu.SMEM)
     anywhere = pl.BlockSpec(memory_space=pl.ANY)
     dma = pltpu.SemaphoreType.DMA
-    message = (width // 128 * count + 16, 128)
+    message = (width // 128 * count, 128)
+    scales = (max(count // 128, 1), 128)
     others = max(tiles - 1, 1)
     return pl.pallas_call(
         functools.partial(image_kernel, (tiles, chips, chunks, width, lines, groups)),
@@ -457,6 +485,8 @@
             pltpu.VMEM((chunks, rows, width), jnp.float32),
             pltpu.VMEM((2, chips, chunks) + message, jnp.int16),
             pltpu.VMEM((2, chips, chunks) + message, jnp.int16),
+            pltpu.VMEM((2, chips, chunks) + scales, jnp.float32),
+            pltpu.VMEM((2, chips, chunks) + scales, jnp.float32),
             pltpu.VMEM((chunks, tiles, 2 * lines, width), jnp.float32),
             pltpu.VMEM((chunks, others, 2 * lines, width), jnp.float32),
             dma,
@@ -468,6 +498,8 @@
             dma((chunks, 2)),
             dma((groups, chunks)),
             dma((groups, chunks)),
+            dma((2, chips, chunks)),
+            dma((2, chips, chunks)),
             dma((2, chips, chunks)),
             dma((2, chips, chunks)),
             dma((others, chunks)),

time: 87.4 us -> 84.9 us (0.971)
  Pallas kernels: 86.6 us -> 84 us
    pallas_call x1, Pallas kernels: 59.1 us -> 57 us  [lines_image(): pl.pallas_call(functools.partial(image_kernel, (tiles, chips, chunks, wid...]
where the time goes in v4:
time: 84.9 us; the launch traced here: 84.7 us
  Pallas kernels  84 us (99%)
    pallas_call x1, Pallas kernels, lines_image(): pl.pallas_call(functools.partial(image_kernel, (tiles, chips, chunks, wid...  57 us
    pallas_call x1, Pallas kernels, focus(): pl.pallas_call(functools.partial(gradient_kernel, count, tiles), out_shap...  22.2 us
    pallas_call x1, Pallas kernels, focus(): pl.pallas_call(correct_kernel, grid=(lines // group,), out_shape=(jax.Sha...  4.86 us

profile of v4, /device:TPU:0, one launch (start us, length us, event | category | flops | bytes accessed | tf_op | source)
XLA Modules:
  0.0 84.7 jit_solution(2422322799911201414)
XLA Ops:
  0.6 57.0 %shard_map.122.image_ref = f32[2,16,8192]{2,1,0:T(8,128)} custom-call(s32[16]{0:T(128)} %offsets_ref.1, f32[4,16]{1,0:T(4,128)} %bitcast.2, bf16[2,1024,128]{2,1,0:T(8,128)(2,1)} %echo_ref.1, bf16[2,4096,1024]{2,1,0:T(8,128)(2,1)} %steer_ref.1), custom_call_target="tpu_custom_call" | custom-call | tf_op jit(solution)/shard_map/pallas_call | solution.py:472
  57.6 22.2 %shard_map.123 = (f32[128,128]{1,0:T(8,128)}, f32[1024,256]{1,0:T(8,128)}) custom-call(s32[16]{0:T(128)} %centers_ref.1, s32[16]{0:T(128)} %halves_ref.1, bf16[128,384]{1,0:T(8,128)(2,1)} %constant.10.clone.down_ref, bf16[768,256]{1,0:T(8,128)(2,1)} %constant.11.clone.over_ref, f32[4,64,128]{2,1,0:T(8,128)} %constant.12.clone.twist_ref, ...), custom_call_target="tpu_custom_call" | custom-call | tf_op jit(solution)/shard_map/pallas_call | solution.py:782
  79.8 4.9 %shard_map.124 = (f32[2,16,8192]{2,1,0:T(8,128)}, f32[64,128]{1,0:T(8,128)}) custom-call(bf16[128,384]{1,0:T(8,128)(2,1)} %constant.13.clone.up_ref, bf16[768,256]{1,0:T(8,128)(2,1)} %constant.14.clone.back_ref, f32[4,64,128]{2,1,0:T(8,128)} %constant.12.clone.twist_ref, f32[128,128]{1,0:T(8,128)} %get-tuple-element.6.total_ref, ...), custom_call_target="tpu_custom_call" | custom-call | tf_op jit(solution)/shard_map/pallas_call | solution.py:803

commit v5 on v4

--- a/solution.py
+++ b/solution.py
@@ -22,6 +22,7 @@
 CORES = 2
 LAG = 3
 EDGE = 32
+SPAN = 512
 
 
 def encode(value, target, scales):
@@ -70,7 +71,7 @@
 
 def image_kernel(
     plan, offsets_ref, taps_hbm, echo_ref, steer_ref, out_ref,
-    taps_ref, held, edge_out, edge_in, left, weights, part, got, away, near, away_scale, near_scale, fin, side,
+    taps_ref, held, edge_out, edge_in, prior, flat, left, weights, part, got, away, near, away_scale, near_scale, fin, side,
     taps_sem, own_sem, edge_send, edge_recv, echo_send, echo_recv, load_sem, pair_send, pair_recv,
     line_send, line_recv, scale_send, scale_recv, side_send, side_recv,
 ):
@@ -112,9 +113,6 @@
             load_sem.at[chunk, half],
         )
 
-    for chunk in range(chunks):
-        for half in range(2):
-            load(chunk, half).start()
 
     def edge():
         return pltpu.make_async_remote_copy(
@@ -135,14 +133,10 @@
         )
 
     if groups > 1:
-        def pack(index, carry):
-            cols = pl.ds(pl.multiple_of(index * 128, 128), 128)
-            for half in range(2):
-                value = turn(unit[columns - EDGE:], echo_ref[half, cols, :])
-                edge_out[half, :, cols] = value.astype(jnp.bfloat16)
-            return carry
-
-        lax.fori_loop(0, pings // 128, pack, 0)
+        for half in range(2):
+            for start in range(0, pings, SPAN):
+                value = turn(unit[columns - EDGE:], echo_ref[half, start:start + SPAN, :])
+                edge_out[half, :, start:start + SPAN] = value.astype(jnp.bfloat16)
 
     reached = len(peers) + 1 + (chip < last).astype(jnp.int32) + (chip > 0).astype(jnp.int32)
     pl.semaphore_wait(barrier, reached)
@@ -163,6 +157,9 @@
         )
         copy.start()
         copies.append(copy)
+    for chunk in range(chunks):
+        for half in range(2):
+            load(chunk, half).start()
     own.wait()
     tap_copy.wait()
     column = lax.broadcasted_iota(jnp.int32, (PBLK, 2 * columns), 1)
@@ -170,11 +167,9 @@
     def interpolate(tile, before):
         def one(index, carry):
             cols = pl.multiple_of(index * 128, 128)
-            turned = []
             for half in range(2):
-                ahead = before(half, cols)
                 value = held[tile, half, pl.ds(cols, 128), :].astype(jnp.float32)
-                value = jnp.concatenate([ahead, value], axis=1)
+                value = jnp.concatenate([before(half, cols).astype(jnp.float32), value], axis=1)
                 blocks = []
                 for inner in range(128 // PBLK):
                     block = index * (128 // PBLK) + inner
@@ -185,8 +180,14 @@
                         moved = pltpu.roll(piece, offset + tap, axis=1)[:, columns:]
                         result = result + taps_ref[tap, block] * moved
                     blocks.append(result)
-                turned.append(turn(unit, jnp.concatenate(blocks, axis=0).astype(jnp.bfloat16)).astype(jnp.bfloat16))
-            real, imag = turned
+                flat[half, pl.ds(cols, 128), :] = jnp.concatenate(blocks, axis=0).astype(jnp.bfloat16)
+            return carry
+
+        lax.fori_loop(0, pings // 128, one, 0, unroll=2)
+        for start in range(0, pings, SPAN):
+            real, imag = [
+                turn(unit, flat[half, start:start + SPAN, :]).astype(jnp.bfloat16) for half in range(2)
+            ]
             for piece in range(columns // lines):
                 row = tile * (columns // lines) + piece
                 owner = row // tiles
@@ -195,19 +196,20 @@
                 place = pl.multiple_of((place * tiles + row % tiles) * 2 * lines, 2 * lines)
                 a = real[piece * lines:(piece + 1) * lines]
                 b = imag[piece * lines:(piece + 1) * lines]
-                left[pl.ds(place, lines), pl.ds(cols, 128)] = a
-                left[pl.ds(place + lines, lines), pl.ds(cols, 128)] = b
-                left[pl.ds(place, lines), pl.ds(pings + cols, 128)] = -b
-                left[pl.ds(place + lines, lines), pl.ds(pings + cols, 128)] = a
-            return carry
-
-        lax.fori_loop(0, pings // 128, one, 0, unroll=2)
+                left[pl.ds(place, lines), start:start + SPAN] = a
+                left[pl.ds(place + lines, lines), start:start + SPAN] = b
+                left[pl.ds(place, lines), pings + start:pings + start + SPAN] = -b
+                left[pl.ds(place + lines, lines), pings + start:pings + start + SPAN] = a
+
+    def unpack():
+        for half in range(2):
+            for start in range(0, pings, 128):
+                value = edge_in[half, :, start:start + 128]
+                value = jnp.concatenate([jnp.zeros((columns - EDGE, 128), jnp.bfloat16), value], axis=0)
+                prior[half, start:start + 128, :] = turn(unit, value).astype(jnp.bfloat16)
 
     def from_edge(half, cols):
-        value = edge_in[half, :, pl.ds(cols, 128)].astype(jnp.float32)
-        value = jnp.where(me > 0, value, 0.0).astype(jnp.bfloat16)
-        value = jnp.concatenate([jnp.zeros((columns - EDGE, 128), jnp.bfloat16), value], axis=0)
-        return turn(unit, value)
+        return prior[half, pl.ds(cols, 128), :]
 
     def from_tile(tile):
         def before(half, cols):
@@ -398,6 +400,11 @@
         @pl.when(me > 0)
         def _():
             edge().wait_recv()
+            unpack()
+
+        @pl.when(me == 0)
+        def _():
+            prior[...] = jnp.zeros_like(prior)
 
         interpolate(me, from_edge)
         steps(me, 0)
@@ -479,6 +486,8 @@
             pltpu.VMEM((tiles, 2, pings, columns), jnp.bfloat16),
             pltpu.VMEM((2, EDGE, pings), jnp.bfloat16),
             pltpu.VMEM((2, EDGE, pings), jnp.bfloat16),
+            pltpu.VMEM((2, pings, columns), jnp.bfloat16),
+            pltpu.VMEM((2, pings, columns), jnp.bfloat16),
             pltpu.VMEM((CORES * rows, 2 * pings), jnp.bfloat16),
             pltpu.VMEM((chunks, width, 2 * pings), jnp.bfloat16),
             pltpu.VMEM((chunks, CORES, rows, width), jnp.float32),

time: 84.9 us -> 83.6 us (0.985)
  Pallas kernels: 84 us -> 82.8 us
    pallas_call x1, Pallas kernels: 57 us -> 55.7 us  [lines_image(): pl.pallas_call(functools.partial(image_kernel, (tiles, chips, chunks, wid...]
where the time goes in v5:
time: 83.6 us; the launch traced here: 83.4 us
  Pallas kernels  82.8 us (99%)
    pallas_call x1, Pallas kernels, lines_image(): pl.pallas_call(functools.partial(image_kernel, (tiles, chips, chunks, wid...  55.7 us
    pallas_call x1, Pallas kernels, focus(): pl.pallas_call(functools.partial(gradient_kernel, count, tiles), out_shap...  22.2 us
    pallas_call x1, Pallas kernels, focus(): pl.pallas_call(correct_kernel, grid=(lines // group,), out_shape=(jax.Sha...  4.86 us

profile of v5, /device:TPU:0, one launch (start us, length us, event | category | flops | bytes accessed | tf_op | source)
XLA Modules:
  0.0 83.4 jit_solution(4972780574605329195)
XLA Ops:
  0.6 55.7 %shard_map.122.image_ref = f32[2,16,8192]{2,1,0:T(8,128)} custom-call(s32[16]{0:T(128)} %offsets_ref.1, f32[4,16]{1,0:T(4,128)} %bitcast.2, bf16[2,1024,128]{2,1,0:T(8,128)(2,1)} %echo_ref.1, bf16[2,4096,1024]{2,1,0:T(8,128)(2,1)} %steer_ref.1), custom_call_target="tpu_custom_call" | custom-call | tf_op jit(solution)/shard_map/pallas_call | solution.py:479
  56.4 22.2 %shard_map.123 = (f32[128,128]{1,0:T(8,128)}, f32[1024,256]{1,0:T(8,128)}) custom-call(s32[16]{0:T(128)} %centers_ref.1, s32[16]{0:T(128)} %halves_ref.1, bf16[128,384]{1,0:T(8,128)(2,1)} %constant.10.clone.down_ref, bf16[768,256]{1,0:T(8,128)(2,1)} %constant.11.clone.over_ref, f32[4,64,128]{2,1,0:T(8,128)} %constant.12.clone.twist_ref, ...), custom_call_target="tpu_custom_call" | custom-call | tf_op jit(solution)/shard_map/pallas_call | solution.py:791
  78.6 4.9 %shard_map.124 = (f32[2,16,8192]{2,1,0:T(8,128)}, f32[64,128]{1,0:T(8,128)}) custom-call(bf16[128,384]{1,0:T(8,128)(2,1)} %constant.13.clone.up_ref, bf16[768,256]{1,0:T(8,128)(2,1)} %constant.14.clone.back_ref, f32[4,64,128]{2,1,0:T(8,128)} %constant.12.clone.twist_ref, f32[128,128]{1,0:T(8,128)} %get-tuple-element.6.total_ref, ...), custom_call_target="tpu_custom_call" | custom-call | tf_op jit(solution)/shard_map/pallas_call | solution.py:812

commit v6 on v5

--- a/solution.py
+++ b/solution.py
@@ -21,7 +21,7 @@
 
 CORES = 2
 LAG = 3
-EDGE = 32
+EDGE = 24
 SPAN = 512
 
 
@@ -521,7 +521,6 @@
 
 
 LANES = 128
-BATCH = 4
 
 
 def split(value):
@@ -591,6 +590,7 @@
 
     lines, length = image_ref.shape[1:]
     high = length // LANES
+    batch = min(lines, 16)
     for half in range(2):
         for row in range(high):
             grid[pl.ds(half * high + row, lines, stride=2 * high), :] = image_ref[
@@ -620,20 +620,20 @@
     def windowed(index, carry):
         numer, denom = carry
         chosen = []
-        for inner in range(BATCH):
-            line = index * BATCH + inner
+        for inner in range(batch):
+            line = index * batch + inner
             distance = cells - centers_ref[line]
             distance = jnp.where(distance < 0, distance + length, distance)
             distance = jnp.minimum(distance, length - distance)
             inside = (distance <= halves_ref[line]).astype(jnp.float32)
             chosen.append(field(line) * jnp.concatenate([inside, inside], axis=0))
         found = spectrum_of(chosen, down_ref, over_ref, twist_ref)
-        for inner in range(BATCH):
+        for inner in range(batch):
             real = found[inner * high:(inner + 1) * high, :LANES]
             imag = found[inner * high:(inner + 1) * high, LANES:]
             next_real = after(real)
             next_imag = after(imag)
-            here = lane == index * BATCH + inner
+            here = lane == index * batch + inner
             cos = jnp.sum(jnp.where(here, turned[0], 0.0), axis=1, keepdims=True)[:1]
             sin = jnp.sum(jnp.where(here, turned[1], 0.0), axis=1, keepdims=True)[:1]
             numer = numer + (real * next_real + imag * next_imag) * sin
@@ -642,7 +642,7 @@
         return numer, denom
 
     zero = jnp.zeros((high, LANES), jnp.float32)
-    numer, denom = lax.fori_loop(0, lines // BATCH, windowed, (zero, zero))
+    numer, denom = lax.fori_loop(0, lines // batch, windowed, (zero, zero))
     each = value.shape[1]
     for block in range(count // 2):
         value[block] = numer[block * each:(block + 1) * each]
@@ -664,12 +664,12 @@
 
     def whole(index, carry):
         found = spectrum_of(
-            [field(index * BATCH + inner) for inner in range(BATCH)], down_ref, over_ref, twist_ref
-        )
-        spec_ref[pl.ds(pl.multiple_of(index * BATCH * high, BATCH * high), BATCH * high), :] = found
+            [field(index * batch + inner) for inner in range(batch)], down_ref, over_ref, twist_ref
+        )
+        spec_ref[pl.ds(pl.multiple_of(index * batch * high, batch * high), batch * high), :] = found
         return carry
 
-    lax.fori_loop(0, lines // BATCH, whole, 0)
+    lax.fori_loop(0, lines // batch, whole, 0)
     total = value[me]
     for step, copy in enumerate(copies):
         copy.wait()
@@ -784,7 +784,7 @@
     cos, sin = waves(high, length, LANES)
     twist = np.stack([cos, sin, cos / length, sin / length]).astype(np.float32)
     each = 2 * high // count
-    group = 8
+    group = lines
     vmem = pl.BlockSpec(memory_space=pltpu.VMEM)
     smem = pl.BlockSpec(memory_space=pltpu.SMEM)
     semaphores = pltpu.SemaphoreType.DMA((count - 1,))

time: 83.6 us -> 81.2 us (0.971)
  Pallas kernels: 82.8 us -> 80.4 us
    pallas_call x1, Pallas kernels: 22.2 us -> 20.9 us  [focus(): pl.pallas_call(functools.partial(gradient_kernel, count, tiles), out_shap...]
where the time goes in v6:
time: 81.2 us; the launch traced here: 81 us
  Pallas kernels  80.4 us (99%)
    pallas_call x1, Pallas kernels, lines_image(): pl.pallas_call(functools.partial(image_kernel, (tiles, chips, chunks, wid...  55 us
    pallas_call x1, Pallas kernels, focus(): pl.pallas_call(functools.partial(gradient_kernel, count, tiles), out_shap...  20.9 us
    pallas_call x1, Pallas kernels, focus(): pl.pallas_call(correct_kernel, grid=(lines // group,), out_shape=(jax.Sha...  4.51 us

profile of v6, /device:TPU:0, one launch (start us, length us, event | category | flops | bytes accessed | tf_op | source)
XLA Modules:
  0.0 81.0 jit_solution(5110819304117834400)
XLA Ops:
  0.6 55.0 %shard_map.122.image_ref = f32[2,16,8192]{2,1,0:T(8,128)} custom-call(s32[16]{0:T(128)} %offsets_ref.1, f32[4,16]{1,0:T(4,128)} %bitcast.2, bf16[2,1024,128]{2,1,0:T(8,128)(2,1)} %echo_ref.1, bf16[2,4096,1024]{2,1,0:T(8,128)(2,1)} %steer_ref.1), custom_call_target="tpu_custom_call" | custom-call | tf_op jit(solution)/shard_map/pallas_call | solution.py:479
  55.7 20.9 %shard_map.123 = (f32[128,128]{1,0:T(8,128)}, f32[1024,256]{1,0:T(8,128)}) custom-call(s32[16]{0:T(128)} %centers_ref.1, s32[16]{0:T(128)} %halves_ref.1, bf16[128,384]{1,0:T(8,128)(2,1)} %constant.10.clone.down_ref, bf16[768,256]{1,0:T(8,128)(2,1)} %constant.11.clone.over_ref, f32[4,64,128]{2,1,0:T(8,128)} %constant.12.clone.twist_ref, ...), custom_call_target="tpu_custom_call" | custom-call | tf_op jit(solution)/shard_map/pallas_call | solution.py:791
  76.5 4.5 %shard_map.124 = (f32[2,16,8192]{2,1,0:T(8,128)}, f32[64,128]{1,0:T(8,128)}) custom-call(bf16[128,384]{1,0:T(8,128)(2,1)} %constant.13.clone.up_ref, bf16[768,256]{1,0:T(8,128)(2,1)} %constant.14.clone.back_ref, f32[4,64,128]{2,1,0:T(8,128)} %constant.12.clone.twist_ref, f32[128,128]{1,0:T(8,128)} %get-tuple-element.6.total_ref, ...), custom_call_target="tpu_custom_call" | custom-call | tf_op jit(solution)/shard_map/pallas_call | solution.py:812

commit v7 on v6

--- a/solution.py
+++ b/solution.py
@@ -85,8 +85,8 @@
     core = lax.axis_index("ping") % CORES
     last = chips - 1
     partner = {"ping": chip * CORES + 1 - core}
-    above = {"ping": (chip + 1) * CORES + core}
-    below = {"ping": (chip - 1) * CORES + core}
+    above = {"ping": lax.min(chip + 1, last) * CORES + core}
+    below = {"ping": lax.max(chip - 1, 0) * CORES + core}
     peers = [{"rng": lax.rem(me + step, tiles)} for step in range(1, tiles)]
 
     barrier = pltpu.get_barrier_semaphore()

time: 81.2 us -> 81.2 us (level)
  no operation moved by 1% of the time
where the time goes in v7:
time: 81.2 us; the launch traced here: 81 us
  Pallas kernels  80.4 us (99%)
    pallas_call x1, Pallas kernels, lines_image(): pl.pallas_call(functools.partial(image_kernel, (tiles, chips, chunks, wid...  55 us
    pallas_call x1, Pallas kernels, focus(): pl.pallas_call(functools.partial(gradient_kernel, count, tiles), out_shap...  20.9 us
    pallas_call x1, Pallas kernels, focus(): pl.pallas_call(correct_kernel, grid=(lines // group,), out_shape=(jax.Sha...  4.51 us

profile of v7, /device:TPU:0, one launch (start us, length us, event | category | flops | bytes accessed | tf_op | source)
XLA Modules:
  0.0 81.0 jit_solution(17664680368437088886)
XLA Ops:
  0.6 55.0 %shard_map.122.image_ref = f32[2,16,8192]{2,1,0:T(8,128)} custom-call(s32[16]{0:T(128)} %offsets_ref.1, f32[4,16]{1,0:T(4,128)} %bitcast.2, bf16[2,1024,128]{2,1,0:T(8,128)(2,1)} %echo_ref.1, bf16[2,4096,1024]{2,1,0:T(8,128)(2,1)} %steer_ref.1), custom_call_target="tpu_custom_call" | custom-call | tf_op jit(solution)/shard_map/pallas_call | solution.py:479
  55.7 20.9 %shard_map.123 = (f32[128,128]{1,0:T(8,128)}, f32[1024,256]{1,0:T(8,128)}) custom-call(s32[16]{0:T(128)} %centers_ref.1, s32[16]{0:T(128)} %halves_ref.1, bf16[128,384]{1,0:T(8,128)(2,1)} %constant.10.clone.down_ref, bf16[768,256]{1,0:T(8,128)(2,1)} %constant.11.clone.over_ref, f32[4,64,128]{2,1,0:T(8,128)} %constant.12.clone.twist_ref, ...), custom_call_target="tpu_custom_call" | custom-call | tf_op jit(solution)/shard_map/pallas_call | solution.py:791
  76.5 4.5 %shard_map.124 = (f32[2,16,8192]{2,1,0:T(8,128)}, f32[64,128]{1,0:T(8,128)}) custom-call(bf16[128,384]{1,0:T(8,128)(2,1)} %constant.13.clone.up_ref, bf16[768,256]{1,0:T(8,128)(2,1)} %constant.14.clone.back_ref, f32[4,64,128]{2,1,0:T(8,128)} %constant.12.clone.twist_ref, f32[128,128]{1,0:T(8,128)} %get-tuple-element.6.total_ref, ...), custom_call_target="tpu_custom_call" | custom-call | tf_op jit(solution)/shard_map/pallas_call | solution.py:812
